TPU v7x, 32 devices: a whole 2x2x4 slice. The times are simulated.
32 devices in a mesh: lat: 4 (over z), lon: 8 (over y, x, core).
Axes of the slice: x: 2, y: 2, z: 4, core: 2. Of those that a mesh axis runs over, the one named last changes fastest.
Arguments:
- observations: bfloat16 [49152, 128], P(('lat', 'lon')), may hold values from -6 to 6
- owner_device: int32 [49152, 1], P(('lat', 'lon')), may hold values from 0 to 31; in each aligned block of 1536 rows (0 to 1535, 1536 to 3071, ...) at most 96 rows name the same one
- local_cell: int32 [49152], P(('lat', 'lon')), may hold values from 0 to 383
- valid_counts: int32 [32], P(('lat', 'lon')), may hold values from 768 to 1536
- weight_in: bfloat16 [128, 256], replicated, may hold values from -0.5 to 0.5
- bias_in: float32 [256], replicated, may hold values from -3 to 3
- weight_out: bfloat16 [256, 256], replicated, may hold values from -0.375 to 0.375
- kernel_taps: float32 [9, 256], replicated, may hold values from -2 to 2
- cotangent: bfloat16 [64, 192, 256], P(('lat', 'lon')), may hold values from -6 to 6
Outputs:
- grid_out: bfloat16 [64, 192, 256], P(('lat', 'lon'))
- grad_weight_in: float32 [128, 256], replicated
- grad_bias_in: float32 [256], replicated
- grad_weight_out: float32 [256, 256], replicated
- grad_kernel: float32 [9, 256], replicated
Inputs may be any that keep to these rules, and one draw needn't show every extreme that they name: `owner_device`: within the rows of one block, at most 96 rows name one owner, and in every draw some block names some owner exactly 96 times.
All inputs are finite; a program needn't handle non-finite values.
Results may differ from a plain program's by a relative error of at most 0.0065.
Values may be sent and summed in bfloat16 or wider, within the bound.
A program may use at most 64 MiB of HBM per device.

v0:
```python
import functools
import math

import jax
import jax.numpy as jnp
from jax import lax
from jax.experimental import pallas as pl
from jax.experimental.pallas import tpu as pltpu
from jax.sharding import PartitionSpec as P

MESH = pl.DeviceIdType.MESH
F32 = jnp.float32
BF16 = jnp.bfloat16
OFFSETS = [(a, b) for a in (-1, 0, 1) for b in (-1, 0, 1)]
CURVE = math.sqrt(2.0 / math.pi)
META = 16
GROUP = 4


def round_up(value, step):
    return -(-value // step) * step


def iota(shape, dim):
    return lax.broadcasted_iota(jnp.int32, shape, dim)


def dot(left, right, contract=((1,), (0,))):
    return lax.dot_general(left, right, (contract, ((), ())), preferred_element_type=F32)


def kernel(
    n_lat, n_lon, slots, piece, scale,
    obs, owner, cell, count, w_in, b_in, w_out, taps, cot,
    grid_o, gin_o, gb_o, gout_o, gk_o,
    meta, slot_row, sbuf, rbuf, cot_top, cot_bot, adj_s, adj_r, adj_f, adj_b,
    dep, dep_b, dep_r, hal_top, hal_bot, strip, total, rounded, parts, gathered, gk_s, gk_lon, gk_lat,
    row_send, row_recv, cot_send, cot_recv, adj_send, adj_recv, dep_send, dep_recv,
    hal_send, hal_recv, sum_send, sum_recv, all_send, all_recv, gk_send, gk_recv,
):
    n = n_lat * n_lon
    lat, lon = lax.axis_index("lat"), lax.axis_index("lon")
    me = lat * n_lon + lon
    obs_rows, feat = obs.shape
    own_rows, cols, channels = cot.shape
    tile_rows = own_rows * n_lon
    tile_cols = cols // n_lon
    cells = tile_rows * tile_cols
    hidden_size = w_in.shape[1]
    groups = n // GROUP
    used = -(-(hidden_size + feat + 16) // piece)

    def place(target):
        return (target // n_lon, lax.rem(target, n_lon))

    def partner(turn):
        return (lax.rem(lat + lax.rem(turn, n_lat), n_lat), lax.rem(lon + turn // n_lat, n_lon))

    def number(turn):
        to_lat, to_lon = partner(turn)
        return to_lat * n_lon + to_lon

    def remote(src, dst, send, recv, device):
        return pltpu.make_async_remote_copy(
            src_ref=src, dst_ref=dst, send_sem=send, recv_sem=recv,
            device_id=device, device_id_type=MESH,
        )

    def drain(ref, sem):
        pltpu.make_async_copy(ref, ref, sem).wait()

    barrier = pltpu.get_barrier_semaphore()

    def greet(off, carry):
        pl.semaphore_signal(
            barrier, inc=1, device_id=place(lax.rem(me + off, n)), device_id_type=MESH
        )
        return carry

    lax.fori_loop(1, n, greet, 0)

    @pl.when(me == 0)
    def _():
        cot_top[...] = jnp.zeros_like(cot_top)

    @pl.when(me == n - 1)
    def _():
        cot_bot[...] = jnp.zeros_like(cot_bot)

    has_top = jnp.logical_and(lon == 0, lat > 0)
    has_bot = jnp.logical_and(lon == n_lon - 1, lat < n_lat - 1)

    @pl.when(jnp.logical_not(has_top))
    def _():
        hal_top[...] = jnp.zeros_like(hal_top)

    @pl.when(jnp.logical_not(has_bot))
    def _():
        hal_bot[...] = jnp.zeros_like(hal_bot)

    dep[...] = jnp.zeros_like(dep)
    total[...] = jnp.zeros_like(total)
    dep_b[0] = jnp.zeros((tile_cols, channels), BF16)
    dep_b[tile_rows + 1] = jnp.zeros((tile_cols, channels), BF16)

    own_row = owner[...]
    match = (own_row == iota((n, obs_rows), 0)).astype(F32)
    block = 256 if obs_rows % 256 == 0 else 128
    upper = (iota((block, block), 0) < iota((block, block), 1)).astype(F32).astype(BF16)
    carry = jnp.zeros((n, 1), F32)
    ranks = []
    for start in range(0, obs_rows, block):
        part = match[:, start:start + block]
        before = dot(part.astype(BF16), upper) + carry
        ranks.append(jnp.sum(before * part, axis=0, keepdims=True))
        carry = carry + jnp.sum(part, axis=1, keepdims=True)
    rank = jnp.concatenate(ranks, axis=1).astype(jnp.int32)
    slot_row[...] = own_row * slots + rank
    lane = iota((1, obs_rows), 1)
    code = jnp.where(lane < count[0], cell[...] + 1, 0)
    high = (code // 128).astype(F32)
    low = lax.rem(code, 128).astype(F32)
    coded = jnp.concatenate([match * high, match * low], axis=0).astype(BF16)
    by_rank = (rank == iota((128, obs_rows), 0)).astype(F32).astype(BF16)
    meta[...] = dot(coded, by_rank, ((1,), (1,)))

    pl.semaphore_wait(barrier, n - 1)

    up_copy = remote(cot.at[own_rows - 1], cot_top, cot_send.at[0], cot_recv.at[0], place(lax.rem(me + 1, n)))
    down_copy = remote(cot.at[0], cot_bot, cot_send.at[1], cot_recv.at[1], place(lax.rem(me + n - 1, n)))

    @pl.when(me < n - 1)
    def _():
        up_copy.start()

    @pl.when(me > 0)
    def _():
        down_copy.start()

    def row_copy(off, g):
        return remote(
            sbuf.at[off], rbuf.at[off], row_send, row_recv.at[g], partner(off)
        )

    def send_group(g, carry, first=False):
        ids = slot_row[...]
        picks = []
        for q in range(GROUP):
            target = number(g * GROUP + q)
            pick = (ids - target * slots) == iota((slots, obs_rows), 0)
            picks.append(pick.astype(F32).astype(BF16))
        rows = dot(jnp.concatenate(picks, axis=0), obs[...]).astype(BF16)
        line = iota((META, 128), 0)
        for q in range(GROUP):
            off = g * GROUP + q
            target = number(off)
            sbuf[off, :slots, :] = rows[q * slots:(q + 1) * slots]
            tail = jnp.where(
                line == 0, meta[pl.ds(target, 1), :],
                jnp.where(line == 1, meta[pl.ds(n + target, 1), :], 0.0),
            )
            sbuf[off, slots:slots + META, :] = tail.astype(BF16)
        for q in range(GROUP):
            if first and q == 0:
                pltpu.make_async_copy(sbuf.at[0], rbuf.at[0], row_recv.at[0]).start()
            else:
                row_copy(g * GROUP + q, g).start()
        return carry

    send_group(0, 0, True)
    lax.fori_loop(1, groups, send_group, 0)

    @pl.when(me > 0)
    def _():
        up_copy.wait_recv()

    @pl.when(me < n - 1)
    def _():
        down_copy.wait_recv()

    tap = taps[...]

    def shifts(row):
        return {0: row, 1: pltpu.roll(row, 1, 0), -1: pltpu.roll(row, cols - 1, 0)}

    cot_rows = [cot_top[...]] + [cot[r] for r in range(own_rows)] + [cot_bot[...]]
    sums = [jnp.zeros((cols, channels), F32) for _ in range(own_rows)]
    for at, row in enumerate(cot_rows):
        moved = shifts(row.astype(F32))
        for y in range(own_rows):
            a = y - (at - 1)
            if abs(a) <= 1:
                for b in (-1, 0, 1):
                    k = 3 * (a + 1) + b + 1
                    sums[y] = sums[y] + tap[k:k + 1] * moved[b]
    for y in range(own_rows):
        value = scale * sums[y]
        for j in range(n_lon):
            adj_s[j, y] = value[j * tile_cols:(j + 1) * tile_cols].astype(BF16)

    def adj_copy(step):
        other = lax.rem(lon + step, n_lon)
        return remote(
            adj_s.at[other], adj_r.at[lon], adj_send, adj_recv, (lat, other)
        )

    for step in range(1, n_lon):
        adj_copy(step).start()
    adj_r[lon] = adj_s[lon]

    drain(adj_r.at[pl.ds(0, n_lon - 1)], adj_recv)
    for k in range(n_lon):
        for y in range(own_rows):
            m = k * own_rows + y
            adj_f[m * tile_cols:(m + 1) * tile_cols, :] = adj_r[k, y].astype(F32)
    adj_b[...] = adj_f[...].astype(BF16)

    bias_at = hidden_size + feat

    def take_group(g, carry):
        held = rbuf.at[pl.ds(g * GROUP, GROUP)]
        drain(held, row_recv.at[g])
        rows = jnp.concatenate([rbuf[g * GROUP + q, :slots, :] for q in range(GROUP)], axis=0)
        same = iota((slots, 128), 0) == iota((slots, 128), 1)
        spread = []
        for q in range(GROUP):
            tail = rbuf[g * GROUP + q, slots:slots + META, :].astype(F32)
            spread.append(jnp.concatenate(
                [jnp.where(same, tail[0:1], 0.0), jnp.where(same, tail[1:2], 0.0)], axis=1
            ).astype(BF16))
        weigh = jnp.where(iota((256, 128), 0) < 128, 128.0, 1.0).astype(BF16)
        codes = dot(jnp.concatenate(spread, axis=0), weigh).astype(jnp.int32)
        lanes = iota(codes.shape, 1) + 1
        pick = jnp.concatenate(
            [(codes == lanes + at).astype(F32).astype(BF16) for at in range(0, cells, 128)], axis=1
        )
        x = dot(rows, w_in[...]) + b_in[...]
        square = x * x
        t = jnp.tanh(CURVE * (x + 0.044715 * (square * x)))
        half = 0.5 * (1.0 + t)
        hidden = (x * half).astype(BF16)
        slope = half + 0.5 * x * (1.0 - t * t) * (CURVE * (1.0 + 3.0 * 0.044715 * square))
        encoded = dot(hidden, w_out[...]).astype(BF16)
        dep[...] += dot(pick, encoded, ((0,), (0,)))
        upstream = dot(pick, adj_b[...]).astype(BF16)
        back = dot(upstream, w_out[...], ((1,), (1,)))
        pre = (back * slope).astype(BF16)
        total[0:hidden_size, :] += dot(hidden, upstream, ((0,), (0,)))
        total[hidden_size:bias_at, :] += dot(rows, pre, ((0,), (0,)))
        total[bias_at:bias_at + 1, :] += jnp.sum(pre.astype(F32), axis=0, keepdims=True)
        return carry

    lax.fori_loop(0, groups, take_group, 0)

    for m in range(tile_rows):
        dep_b[m + 1] = dep[m * tile_cols:(m + 1) * tile_cols, :].astype(BF16)

    def dep_copy(step):
        other = lax.rem(lon + step, n_lon)
        return remote(
            dep_b.at[pl.ds(other * own_rows, own_rows + 2)], dep_r.at[lon],
            dep_send, dep_recv, (lat, other),
        )

    low_copy = remote(
        dep_b.at[tile_rows], hal_top.at[lon], hal_send.at[0], hal_recv.at[0],
        (lax.rem(lat + 1, n_lat), 0),
    )
    high_copy = remote(
        dep_b.at[1], hal_bot.at[lon], hal_send.at[1], hal_recv.at[1],
        (lax.rem(lat + n_lat - 1, n_lat), n_lon - 1),
    )

    @pl.when(lat < n_lat - 1)
    def _():
        low_copy.start()

    @pl.when(lat > 0)
    def _():
        high_copy.start()

    for step in range(1, n_lon):
        dep_copy(step).start()
    dep_r[lon] = dep_b[pl.ds(lon * own_rows, own_rows + 2)]

    def span(at):
        return pl.ds(pl.multiple_of(at * piece, 16), piece)

    def sum_start(off, carry):
        target = number(off)

        @pl.when(target < used)
        def _():
            remote(
                rounded.at[span(target)], parts.at[off - 1], sum_send, sum_recv, partner(off)
            ).start()

        return carry

    rounded[...] = total[...].astype(BF16)
    lax.fori_loop(1, n, sum_start, 0)

    drain(dep_r.at[pl.ds(0, n_lon - 1)], dep_recv)

    @pl.when(has_top)
    def _():
        drain(hal_top, hal_recv.at[0])

    @pl.when(has_bot)
    def _():
        drain(hal_bot, hal_recv.at[1])

    for j in range(n_lon):
        for r in range(own_rows + 2):
            value = dep_r[j, r].astype(F32)
            if r == 0:
                value = value + hal_top[j].astype(F32)
            if r == own_rows + 1:
                value = value + hal_bot[j].astype(F32)
            strip[r, j * tile_cols:(j + 1) * tile_cols, :] = value

    fields = [jnp.zeros((cols, channels), F32) for _ in range(own_rows)]
    kernel_rows = [jnp.zeros((1, channels), F32) for _ in OFFSETS]
    for at in range(own_rows + 2):
        moved = shifts(strip[at])
        for y in range(own_rows):
            a = at - 1 - y
            if abs(a) <= 1:
                for b in (-1, 0, 1):
                    k = 3 * (a + 1) + b + 1
                    fields[y] = fields[y] + tap[k:k + 1] * moved[-b]
                    kernel_rows[k] = kernel_rows[k] + jnp.sum(
                        cot[y].astype(F32) * moved[-b], axis=0, keepdims=True
                    )
    for y in range(own_rows):
        grid_o[y] = fields[y].astype(BF16)
    spare = gk_s.shape[1] - len(OFFSETS)
    grad_taps = scale * jnp.concatenate(kernel_rows + [jnp.zeros((spare, channels), F32)], axis=0)
    gk_s[0] = grad_taps.astype(BF16)
    for step in range(1, n_lon):
        remote(
            gk_s.at[0], gk_lon.at[lon], gk_send.at[0], gk_recv.at[0],
            (lat, lax.rem(lon + step, n_lon)),
        ).start()

    @pl.when(me < used)
    def _():
        drain(parts, sum_recv)

        def add_part(at, value):
            return value + parts[at].astype(F32)

        gathered[span(me), :] = lax.fori_loop(
            0, n - 1, add_part, total[span(me), :]
        ).astype(BF16)

        def all_start(off, carry):
            remote(
                gathered.at[span(me)], gathered.at[span(me)], all_send, all_recv, partner(off)
            ).start()
            return carry

        lax.fori_loop(1, n, all_start, 0)

    gk_lon[lon] = gk_s[0]
    drain(gk_lon.at[pl.ds(0, n_lon - 1)], gk_recv.at[0])
    grad_taps = gk_lon[0].astype(F32)
    for at in range(1, n_lon):
        grad_taps = grad_taps + gk_lon[at].astype(F32)
    gk_s[1] = grad_taps.astype(BF16)
    for step in range(1, n_lat):
        remote(
            gk_s.at[1], gk_lat.at[lat], gk_send.at[1], gk_recv.at[1],
            (lax.rem(lat + step, n_lat), lon),
        ).start()
    gk_lat[lat] = gk_s[1]
    drain(gk_lat.at[pl.ds(0, n_lat - 1)], gk_recv.at[1])
    grad_taps = gk_lat[0].astype(F32)
    for at in range(1, n_lat):
        grad_taps = grad_taps + gk_lat[at].astype(F32)
    gk_o[...] = grad_taps[0:len(OFFSETS)]

    @pl.when(me < used)
    def _():
        drain(gathered.at[pl.ds(0, (used - 1) * piece)], all_recv)

    @pl.when(me >= used)
    def _():
        drain(gathered.at[pl.ds(0, used * piece)], all_recv)

    gout_o[...] = gathered[0:hidden_size, :].astype(F32)
    gin_o[...] = gathered[hidden_size:bias_at, :].astype(F32)
    gb_o[...] = gathered[bias_at:bias_at + 16, :].astype(F32)[0:1]

    drain(sbuf.at[pl.ds(0, n - 1)], row_send)
    drain(adj_s.at[pl.ds(0, n_lon - 1)], adj_send)
    drain(dep_r.at[pl.ds(0, n_lon - 1)], dep_send)
    drain(gk_lon.at[pl.ds(0, n_lon - 1)], gk_send.at[0])
    drain(gk_lat.at[pl.ds(0, n_lat - 1)], gk_send.at[1])

    @pl.when(me < used)
    def _():
        drain(gathered.at[pl.ds(0, (used - 1) * piece)], sum_send)
        drain(gathered.at[pl.ds(0, (n - 1) * piece)], all_send)

    @pl.when(me >= used)
    def _():
        drain(gathered.at[pl.ds(0, used * piece)], sum_send)

    @pl.when(me < n - 1)
    def _():
        up_copy.wait_send()

    @pl.when(me > 0)
    def _():
        down_copy.wait_send()

    @pl.when(lat < n_lat - 1)
    def _():
        low_copy.wait_send()

    @pl.when(lat > 0)
    def _():
        high_copy.wait_send()


def local(
    observations, owner_device, local_cell, valid_counts,
    weight_in, bias_in, weight_out, kernel_taps, cotangent,
):
    n_lat, n_lon = lax.axis_size("lat"), lax.axis_size("lon")
    n = n_lat * n_lon
    obs_rows, feat = observations.shape
    hidden_size, channels = weight_out.shape
    own_rows, cols, _ = cotangent.shape
    tile_rows, tile_cols = own_rows * n_lon, cols // n_lon
    cells = tile_rows * tile_cols
    slots = round_up(2 * obs_rows // n, 16)
    piece = round_up(-(-(hidden_size + feat + 16) // n), 16)
    taps = kernel_taps.shape[0]
    kernel_pad = round_up(taps, 16)
    scale = 1.0 / math.sqrt(obs_rows * n)
    vmem = pl.BlockSpec(memory_space=pltpu.VMEM)
    dma = pltpu.SemaphoreType.DMA
    out = pl.pallas_call(
        functools.partial(kernel, n_lat, n_lon, slots, piece, scale),
        out_shape=(
            jax.ShapeDtypeStruct(cotangent.shape, BF16),
            jax.ShapeDtypeStruct((feat, hidden_size), F32),
            jax.ShapeDtypeStruct((1, hidden_size), F32),
            jax.ShapeDtypeStruct((hidden_size, channels), F32),
            jax.ShapeDtypeStruct((taps, channels), F32),
        ),
        in_specs=[vmem, vmem, vmem, pl.BlockSpec(memory_space=pltpu.SMEM)] + [vmem] * 5,
        out_specs=(vmem,) * 5,
        scratch_shapes=[
            pltpu.VMEM((2 * n, 128), F32),
            pltpu.VMEM((1, obs_rows), jnp.int32),
            pltpu.VMEM((n, slots + META, feat), BF16),
            pltpu.VMEM((n, slots + META, feat), BF16),
            pltpu.VMEM((cols, channels), BF16),
            pltpu.VMEM((cols, channels), BF16),
            pltpu.VMEM((n_lon, own_rows, tile_cols, channels), BF16),
            pltpu.VMEM((n_lon, own_rows, tile_cols, channels), BF16),
            pltpu.VMEM((cells, channels), F32),
            pltpu.VMEM((cells, channels), BF16),
            pltpu.VMEM((cells, channels), F32),
            pltpu.VMEM((tile_rows + 2, tile_cols, channels), BF16),
            pltpu.VMEM((n_lon, own_rows + 2, tile_cols, channels), BF16),
            pltpu.VMEM((n_lon, tile_cols, channels), BF16),
            pltpu.VMEM((n_lon, tile_cols, channels), BF16),
            pltpu.VMEM((own_rows + 2, cols, channels), F32),
            pltpu.VMEM((n * piece, channels), F32),
            pltpu.VMEM((n * piece, channels), BF16),
            pltpu.VMEM((n - 1, piece, channels), BF16),
            pltpu.VMEM((n * piece, channels), BF16),
            pltpu.VMEM((2, kernel_pad, channels), BF16),
            pltpu.VMEM((n_lon, kernel_pad, channels), BF16),
            pltpu.VMEM((n_lat, kernel_pad, channels), BF16),
            dma, dma((n // GROUP,)), dma((2,)), dma((2,)), dma, dma, dma, dma,
            dma((2,)), dma((2,)), dma, dma, dma, dma, dma((2,)), dma((2,)),
        ],
        compiler_params=pltpu.CompilerParams(
            collective_id=0, has_side_effects=True, vmem_limit_bytes=60 * 1024 * 1024
        ),
    )(
        observations, owner_device.reshape(1, obs_rows), local_cell.reshape(1, obs_rows),
        valid_counts, weight_in, bias_in.reshape(1, hidden_size), weight_out, kernel_taps, cotangent,
    )
    grid_out, grad_in, grad_bias, grad_out, grad_kernel = out
    return (grid_out, grad_in, grad_bias.reshape(hidden_size), grad_out, grad_kernel)


def solution(mesh):
    return jax.shard_map(
        local,
        mesh=mesh,
        in_specs=(
            P(("lat", "lon"), None),
            P(("lat", "lon"), None),
            P(("lat", "lon")),
            P(("lat", "lon")),
            P(),
            P(),
            P(),
            P(),
            P(("lat", "lon"), None, None),
        ),
        out_specs=(P(("lat", "lon"), None, None), P(), P(), P(), P()),
        check_vma=False,
    )
```

profile of v0, /device:TPU:0, one launch (start us, length us, event | category | flops | bytes accessed | tf_op | source)
XLA Modules:
  0.0 56.2 jit_solution(4822926630827351619)
XLA Ops:
  1.3 1.3 %reshape.23.cell = s32[1,1536]{1,0:T(1,128)} reshape(s32[1536]{0:T(1024)} %param.11) | data formatting | bytes 12288 | tf_op jit(solution)/shard_map/reshape | solution.py:487
  2.6 49.4 %shard_map.128 = (bf16[2,192,256]{2,1,0:T(8,128)(2,1)}, f32[128,256]{1,0:T(8,128)}, f32[1,256]{1,0:T(1,128)}, f32[256,256]{1,0:T(8,128)}, f32[9,256]{1,0:T(8,128)}) custom-call(bf16[1536,128]{1,0:T(8,128)(2,1)} %obs.1, s32[1,1536]{1,0:T(1,128)} %bitcast.3, s32[1,1536]{1,0:T(1,128)} %reshape.23.cell, s32[1]{0:T(128)S(6)} %copy.19.count, ...), custom_call_target="tpu_custom_call" | custom-call | tf_op jit(solution)/shard_map/pallas_call | solution.py:445
  52.0 0.0 copy-start.1
  52.0 0.0 copy-start
  52.0 1.7 %copy.20 = bf16[2,192,256]{2,1,0:T(8,128)(2,1)} copy(bf16[2,192,256]{2,1,0:T(8,128)(2,1)} %get-tuple-element.20) | data formatting | bytes 393216
  53.7 0.0 copy-done.1
  53.7 0.0 copy-start.3
  53.7 0.7 %copy.21 = f32[128,256]{1,0:T(8,128)} copy(f32[128,256]{1,0:T(8,128)S(1)} %copy-done.1) | data formatting | bytes 262144
  54.3 0.0 copy-done.3
  54.3 0.6 %copy.22 = f32[256]{0:T(256)} copy(f32[256]{0:T(256)S(1)} %bitcast.5) | data formatting | bytes 2048
  54.9 0.0 copy-done
  54.9 0.0 copy-start.2
  54.9 0.7 %copy.23 = f32[256,256]{1,0:T(8,128)} copy(f32[256,256]{1,0:T(8,128)S(1)} %copy-done) | data formatting | bytes 524288
  55.6 0.0 copy-done.2
  55.6 0.6 %copy.24 = f32[9,256]{1,0:T(8,128)} copy(f32[9,256]{1,0:T(8,128)S(1)} %copy-done.2) | data formatting | bytes 18432
Async XLA Ops:
  52.0 1.7 %copy-start.1 = (f32[128,256]{1,0:T(8,128)S(1)}, f32[128,256]{1,0:T(8,128)}, u32[]{:S(2)}) copy-start(f32[128,256]{1,0:T(8,128)} %get-tuple-element.21) | copy-start | bytes 393220
  52.0 2.9 %copy-start = (f32[256,256]{1,0:T(8,128)S(1)}, f32[256,256]{1,0:T(8,128)}, u32[]{:S(2)}) copy-start(f32[256,256]{1,0:T(8,128)} %get-tuple-element.23) | copy-start | bytes 786436
  53.7 0.7 %copy-start.3 = (f32[1,256]{1,0:T(1,128)S(1)}, f32[1,256]{1,0:T(1,128)}, u32[]{:S(2)}) copy-start(f32[1,256]{1,0:T(1,128)} %get-tuple-element.12) | copy-start | bytes 3076
  54.9 0.7 %copy-start.2 = (f32[9,256]{1,0:T(8,128)S(1)}, f32[9,256]{1,0:T(8,128)}, u32[]{:S(2)}) copy-start(f32[9,256]{1,0:T(8,128)} %get-tuple-element.24) | copy-start | bytes 27652
where the time goes:
time: 56.6 us; the launch traced here: 56.2 us
  Pallas kernels  49.4 us (87%)
  local copies, waits for them, and re-layouts  5.51 us (10%)
  between operations  1.31 us (2%)
    pallas_call x1, Pallas kernels, local(): pl.pallas_call(functools.partial(kernel, n_lat, n_lon, slots, piece, scal...  49.4 us
    unnamed x13, local copies, waits for them, and re-layouts  4.22 us
    reshape x1, local copies, waits for them, and re-layouts, local(): local_cell.reshape(1, obs_rows)  1.3 us

commit v1 on v0

v1 whole, which is shorter than its diff:
```python
import functools
import math

import jax
import jax.numpy as jnp
from jax import lax
from jax.experimental import pallas as pl
from jax.experimental.pallas import tpu as pltpu
from jax.sharding import PartitionSpec as P

MESH = pl.DeviceIdType.MESH
F32 = jnp.float32
BF16 = jnp.bfloat16
OFFSETS = [(a, b) for a in (-1, 0, 1) for b in (-1, 0, 1)]
CURVE = math.sqrt(2.0 / math.pi)
BEND = 0.044715
META = 8
EDGE = 8
STEP_ROWS = 384
EARLY = 4


def round_up(value, step):
    return -(-value // step) * step


def iota(shape, dim):
    return lax.broadcasted_iota(jnp.int32, shape, dim)


def dot(left, right, contract=((1,), (0,))):
    return lax.dot_general(left, right, (contract, ((), ())), preferred_element_type=F32)


def split_of(n_lat):
    return 2 if n_lat % 2 == 0 and n_lat >= 4 else 1


def kernel(
    n_lat, n_lon, split, slots, batch, scale,
    obs_h, owner_h, cell_h, count, w_in_h, b_in_h, w_out_h, taps_h, cot_h,
    main_o, top_o, bot_o, sums_o, misc_o,
    obs, owner, cell, w_in, b_in, w_out, taps, cot,
    meta, slot_row, sbuf, rbuf, cot_s, cot_e, cot_r, cot_top, cot_bot, c32, adj_f, adj_b,
    dep, moved, con_s, con_e, gka, total, bias, tot_b, rs_r, z_s, z_r, fin_s, misc_s, misc_r, misc_z,
    in_sem, row_send, row_recv, cot_send, cot_recv, edge_send, top_recv, bot_recv,
    con_send, con_recv, rim_send, rim_recv, rs_send, rs_recv, z_send, z_recv, ag_send, ag_recv,
    mp_send, mp_recv, mz_send, mz_recv,
):
    n = n_lat * n_lon
    lat, lon = lax.axis_index("lat"), lax.axis_index("lon")
    me = lat * n_lon + lon
    deep = n_lat // split
    group, level = lat // deep, lax.rem(lat, deep)
    peers = n // split
    obs_rows, feat = obs.shape
    own_rows, cols, channels = cot.shape
    tile_rows, tile_cols = own_rows * n_lon, cols // n_lon
    cells = tile_rows * tile_cols
    wide = tile_cols + EDGE
    hidden_size = w_in.shape[1]
    piece = tot_b.shape[1]
    holders = split * n_lon
    scope = jax.named_scope

    def place(target):
        return (target // n_lon, lax.rem(target, n_lon))

    def partner(off):
        return (group * deep + lax.rem(level + lax.rem(off, deep), deep), lax.rem(lon + off // deep, n_lon))

    def tile_lat(h):
        return h * deep + level

    def remote(src, dst, send, recv, device):
        return pltpu.make_async_remote_copy(
            src_ref=src, dst_ref=dst, send_sem=send, recv_sem=recv,
            device_id=device, device_id_type=MESH,
        )

    def drain(ref, sem):
        pltpu.make_async_copy(ref, ref, sem).wait()

    pairs = [
        (owner_h, owner), (cell_h, cell), (obs_h, obs), (cot_h, cot),
        (w_in_h, w_in), (b_in_h, b_in), (w_out_h, w_out), (taps_h, taps),
    ]
    fetches = [pltpu.make_async_copy(src, dst, in_sem.at[i]) for i, (src, dst) in enumerate(pairs)]
    for fetch in fetches:
        fetch.start()

    barrier = pltpu.get_barrier_semaphore()

    def greet(off, carry):
        pl.semaphore_signal(
            barrier, inc=1, device_id=place(lax.rem(me + off, n)), device_id_type=MESH
        )
        return carry

    with scope("greet"):
        lax.fori_loop(1, n, greet, 0)

    with scope("zero"):
        for h in range(split):
            @pl.when(tile_lat(h) == 0)
            def _(h=h):
                cot_top[h] = jnp.zeros((wide, channels), BF16)

            @pl.when(tile_lat(h) == n_lat - 1)
            def _(h=h):
                cot_bot[h] = jnp.zeros((wide, channels), BF16)

            for b in range(3):
                for i in (0, 1, tile_rows + 2, tile_rows + 3):
                    moved[h, b, i] = jnp.zeros((wide, channels), F32)

        has_top = jnp.logical_and(lon == 0, lat > 0)
        has_bot = jnp.logical_and(lon == n_lon - 1, lat < n_lat - 1)

        @pl.when(jnp.logical_not(has_top))
        def _():
            top_o[...] = jnp.zeros_like(top_o)

        @pl.when(jnp.logical_not(has_bot))
        def _():
            bot_o[...] = jnp.zeros_like(bot_o)

        dep[...] = jnp.zeros_like(dep)
        total[...] = jnp.zeros_like(total)
        bias[...] = jnp.zeros_like(bias)
        gka[...] = jnp.zeros_like(gka)

    with scope("meta"):
        fetches[0].wait()
        own_row = owner[...]
        match = (own_row == iota((n, obs_rows), 0)).astype(F32)
        block = 256 if obs_rows % 256 == 0 else 128
        upper = (iota((block, block), 0) < iota((block, block), 1)).astype(F32).astype(BF16)
        carry = jnp.zeros((n, 1), F32)
        ranks = []
        for start in range(0, obs_rows, block):
            part = match[:, start:start + block]
            before = dot(part.astype(BF16), upper) + carry
            ranks.append(jnp.sum(before * part, axis=0, keepdims=True))
            carry = carry + jnp.sum(part, axis=1, keepdims=True)
        rank = jnp.concatenate(ranks, axis=1).astype(jnp.int32)
        slot_row[...] = own_row * slots + rank
        fetches[1].wait()
        lane = iota((1, obs_rows), 1)
        cells_row = jnp.concatenate([cell[i:i + 1, :] for i in range(obs_rows // 128)], axis=1)
        code = jnp.where(lane < count[0], cells_row + 1, 0)
        high = (code // 128).astype(F32)
        low = lax.rem(code, 128).astype(F32)
        coded = jnp.concatenate([match * high, match * low], axis=0).astype(BF16)
        by_rank = (rank == iota((128, obs_rows), 0)).astype(F32).astype(BF16)
        meta[...] = dot(coded, by_rank, ((1,), (1,)))
        fetches[2].wait()

    per_step = batch // split
    steps = peers // per_step

    def prepare(s, carry):
        ids = slot_row[...]
        picks = []
        for u in range(batch):
            to_lat, to_lon = partner(s * per_step + u // split)
            target = ((u % split) * deep + lax.rem(to_lat, deep)) * n_lon + to_lon
            rel = jnp.clip(ids - target * slots, -1, slots).astype(F32)
            rel = jnp.broadcast_to(rel, (16, obs_rows)).astype(BF16)
            for at in range(0, slots, 16):
                line = (iota((16, obs_rows), 0) + at).astype(F32).astype(BF16)
                picks.append(jnp.where(rel == line, jnp.ones_like(line), jnp.zeros_like(line)))
        rows = dot(jnp.concatenate(picks, axis=0), obs[...]).astype(BF16)
        line = iota((META, 128), 0)
        for q in range(per_step):
            off = s * per_step + q
            to_lat, to_lon = partner(off)
            tail = jnp.zeros((META, 128), F32)
            for h in range(split):
                target = (h * deep + lax.rem(to_lat, deep)) * n_lon + to_lon
                u = q * split + h
                sbuf[off, h * slots:(h + 1) * slots, :] = rows[u * slots:(u + 1) * slots]
                tail = jnp.where(line == 2 * h, meta[pl.ds(target, 1), :], tail)
                tail = jnp.where(line == 2 * h + 1, meta[pl.ds(n + target, 1), :], tail)
            sbuf[off, split * slots:split * slots + META, :] = tail.astype(BF16)
        return carry

    takers = batch

    def ship_one(off):
        remote(sbuf.at[off], rbuf.at[off], row_send, row_recv.at[off // takers], partner(off)).start()

    def ship(s, carry):
        for q in range(per_step):
            ship_one(s * per_step + q)
        return carry

    early = min(EARLY, steps)
    with scope("prep0"):
        lax.fori_loop(0, early, prepare, 0)

    with scope("cotprep"):
        fetches[3].wait()
        rim = iota((EDGE, channels), 0)
        rows_f = [cot[y].astype(F32) for y in range(own_rows)]
        for j in range(n_lon):
            start, stop = j * tile_cols, (j + 1) * tile_cols
            after, ahead = stop % cols, (start - EDGE) % cols
            mixed = jnp.zeros((EDGE, channels), F32)
            for y in range(own_rows):
                row = rows_f[y]
                ends = jnp.where(
                    rim == 0, row[after:after + EDGE],
                    jnp.where(rim == EDGE - 1, row[ahead:ahead + EDGE], 0.0),
                )
                cot_s[j, y * tile_cols:(y + 1) * tile_cols, :] = cot[y, start:stop, :]
                mixed = mixed + (pltpu.roll(ends, EDGE - 2 * y, 0) if y else ends)
                if y == 0:
                    cot_e[0, j, 0:tile_cols, :] = cot[y, start:stop, :]
                    cot_e[0, j, tile_cols:wide, :] = ends.astype(BF16)
                if y == own_rows - 1:
                    cot_e[1, j, 0:tile_cols, :] = cot[y, start:stop, :]
                    cot_e[1, j, tile_cols:wide, :] = ends.astype(BF16)
            cot_s[j, own_rows * tile_cols:own_rows * tile_cols + EDGE, :] = mixed.astype(BF16)

    with scope("barw"):
        pl.semaphore_wait(barrier, n - 1)

    def hop(step):
        return lax.rem(lon + step, n_lon)

    def side(turn):
        return lax.rem(group + turn, split)

    with scope("ship"):
        for turn in range(split - 1, -1, -1):
            to_lat = side(turn) * deep + level
            for step in range(n_lon):
                if turn or step:
                    other = hop(step)
                    remote(
                        cot_s.at[other], cot_r.at[group * n_lon + lon], cot_send, cot_recv, (to_lat, other)
                    ).start()
        cot_r[group * n_lon + lon] = cot_s[lon]

        @pl.when(jnp.logical_and(lon == n_lon - 1, lat < n_lat - 1))
        def _():
            to_tile = lat + 1
            for turn in range(split):
                for j in range(n_lon):
                    remote(
                        cot_e.at[1, j], cot_top.at[to_tile // deep], edge_send, top_recv.at[to_tile // deep],
                        (turn * deep + lax.rem(to_tile, deep), j),
                    ).start()

        @pl.when(jnp.logical_and(lon == 0, lat > 0))
        def _():
            to_tile = lat - 1
            for turn in range(split):
                for j in range(n_lon):
                    remote(
                        cot_e.at[0, j], cot_bot.at[to_tile // deep], edge_send, bot_recv.at[to_tile // deep],
                        (turn * deep + lax.rem(to_tile, deep), j),
                    ).start()

        pltpu.make_async_copy(sbuf.at[0], rbuf.at[0], row_recv.at[0]).start()
        for q in range(1, per_step):
            ship_one(q)
        lax.fori_loop(1, early, ship, 0)

    with scope("prep1"):
        if early < steps:
            lax.fori_loop(early, steps, lambda s, c: ship(s, prepare(s, c)), 0)

    with scope("cotwait"):
        for fetch in fetches[4:]:
            fetch.wait()
        drain(cot_r.at[pl.ds(0, holders - 1)], cot_recv)
        for h in range(split):
            @pl.when(tile_lat(h) > 0)
            def _(h=h):
                drain(cot_top.at[h], top_recv.at[h])

            @pl.when(tile_lat(h) < n_lat - 1)
            def _(h=h):
                drain(cot_bot.at[h], bot_recv.at[h])

    with scope("adjoint"):
        tap = taps[...]
        half = channels // 2
        for h in range(split):
            c32[h, 0] = cot_top[h].astype(F32)
            c32[h, tile_rows + 1] = cot_bot[h].astype(F32)

            def widen(j, carry, h=h):
                at = h * n_lon + j
                ends = cot_r[at, own_rows * tile_cols:own_rows * tile_cols + EDGE, :].astype(F32)
                for r in range(own_rows):
                    m = j * own_rows + r + 1
                    c32[h, m, 0:tile_cols, :] = cot_r[at, r * tile_cols:(r + 1) * tile_cols, :].astype(F32)
                    c32[h, m, tile_cols:wide, :] = pltpu.roll(ends, 2 * r, 0) if r else ends
                return carry

            lax.fori_loop(0, n_lon, widen, 0)

            def adjoin(m, carry, h=h):
                for c in range(0, channels, half):
                    acc = jnp.zeros((tile_cols, half), F32)
                    for a in (-1, 0, 1):
                        row = c32[h, m + 1 - a, :, c:c + half]
                        for b in (-1, 0, 1):
                            k = 3 * (a + 1) + b + 1
                            turned = pltpu.roll(row, b % wide, 0) if b else row
                            acc = acc + tap[k:k + 1, c:c + half] * turned[0:tile_cols]
                    adj_f[pl.ds(pl.multiple_of(m * tile_cols, 8), tile_cols), c:c + half] = scale * acc
                return carry

            lax.fori_loop(0, tile_rows, adjoin, 0)
            adj_b[h] = adj_f[...].astype(BF16)

    def take(t, carry):
        first = t * takers
        with scope("rowwait"):
            drain(rbuf.at[pl.ds(first, takers)], row_recv.at[t])
        rows = jnp.concatenate(
            [rbuf[first + q, h * slots:(h + 1) * slots, :] for h in range(split) for q in range(takers)], axis=0
        )
        x = dot(rows, w_in[...]) + b_in[...]
        square = x * x
        t_val = jnp.tanh(x * (CURVE + (CURVE * BEND) * square))
        upper_half = 0.5 + 0.5 * t_val
        lower_half = 0.5 - 0.5 * t_val
        active = x * upper_half
        hidden = active.astype(BF16)
        slope = upper_half + (active * lower_half) * (2.0 * CURVE + (6.0 * CURVE * BEND) * square)
        encoded = dot(hidden, w_out[...]).astype(BF16)
        share = takers * slots
        ups = []
        for h in range(split):
            codes = []
            for q in range(takers):
                tail = rbuf[first + q, split * slots:split * slots + META, :].astype(F32)
                codes.append((128.0 * tail[2 * h:2 * h + 1] + tail[2 * h + 1:2 * h + 2])[:, 0:slots])
            codes = jnp.concatenate(codes, axis=1).astype(jnp.int32)
            pick = (codes == iota((cells, share), 0) + 1).astype(F32).astype(BF16)
            dep[h] += dot(pick, encoded[h * share:(h + 1) * share])
            ups.append(dot(pick, adj_b[h], ((0,), (0,))).astype(BF16))
        upstream = jnp.concatenate(ups, axis=0)
        back = dot(upstream, w_out[...], ((1,), (1,)))
        pre = (back * slope).astype(BF16)
        total[0:hidden_size, :] += dot(hidden, upstream, ((0,), (0,)))
        total[hidden_size:hidden_size + feat, :] += dot(rows, pre, ((0,), (0,)))
        bias[...] += jnp.sum(pre.astype(F32), axis=0, keepdims=True)
        return carry

    with scope("take"):
        lax.fori_loop(0, peers // takers, take, 0)

    with scope("rssend"):
        for p in range(n_lon):
            tot_b[p] = total[p * piece:(p + 1) * piece, :].astype(BF16)
        for step in range(1, n_lon):
            remote(tot_b.at[hop(step)], rs_r.at[lon], rs_send, rs_recv, (lat, hop(step))).start()

    def spread(h):
        def turn_row(m, carry):
            row = dep[h, pl.ds(pl.multiple_of(m * tile_cols, 8), tile_cols), :]
            row = jnp.concatenate([row, jnp.zeros((EDGE, channels), F32)], axis=0)
            moved[h, 0, m + 2] = pltpu.roll(row, 1, 0)
            moved[h, 1, m + 2] = row
            moved[h, 2, m + 2] = pltpu.roll(row, wide - 1, 0)
            return carry

        lax.fori_loop(0, tile_rows, turn_row, 0)

        def out_row(i, c):
            acc = jnp.zeros((wide, half), F32)
            seen = c32[h, i, :, c:c + half]
            for a in (-1, 0, 1):
                for b in (-1, 0, 1):
                    k = 3 * (a + 1) + b + 1
                    value = moved[h, b + 1, i + 1 + a, :, c:c + half]
                    acc = acc + tap[k:k + 1, c:c + half] * value
                    prod = seen * value
                    folded = prod[0:8]
                    for at in range(8, wide, 8):
                        folded = folded + prod[at:at + 8]
                    gka[k, :, c:c + half] += folded
            return acc

        def strip(j, carry):
            for c in range(0, channels, half):
                mixed = jnp.zeros((EDGE, half), F32)
                for r in range(own_rows):
                    acc = out_row(j * own_rows + r + 1, c)
                    con_s[h, j, r * tile_cols:(r + 1) * tile_cols, c:c + half] = acc[0:tile_cols].astype(BF16)
                    ends = acc[tile_cols:wide]
                    mixed = mixed + (pltpu.roll(ends, EDGE - 2 * r, 0) if r else ends)
                con_s[h, j, own_rows * tile_cols:own_rows * tile_cols + EDGE, c:c + half] = mixed.astype(BF16)
            return carry

        for e, i in ((0, 0), (1, tile_rows + 1)):
            for c in range(0, channels, half):
                con_e[h, e, :, c:c + half] = out_row(i, c).astype(BF16)
        lax.fori_loop(0, n_lon, strip, 0)

    def send_strip(h, step):
        other = hop(step)
        remote(
            con_s.at[h, other], main_o.at[group * n_lon + lon], con_send, con_recv, (tile_lat(h), other)
        ).start()

    def rim_copy(h, e):
        where = group * n_lon + lon
        if e == 0:
            return remote(con_e.at[h, 0], bot_o.at[where], rim_send, rim_recv.at[0], (tile_lat(h) - 1, n_lon - 1))
        return remote(con_e.at[h, 1], top_o.at[where], rim_send, rim_recv.at[1], (tile_lat(h) + 1, 0))

    def send_rims(h):
        @pl.when(tile_lat(h) > 0)
        def _():
            rim_copy(h, 0).start()

        @pl.when(tile_lat(h) < n_lat - 1)
        def _():
            rim_copy(h, 1).start()

    first_part = n_lon // 2
    with scope("spread"):
        for turn in range(1, split):
            h = side(turn)
            spread(h)
            send_rims(h)
            for step in range(first_part):
                send_strip(h, step)
        spread(group)
        send_rims(group)

    with scope("misc"):
        grads = [jnp.sum(gka[k], axis=0, keepdims=True) * scale for k in range(len(OFFSETS))]
        spare = misc_s.shape[0] - len(OFFSETS) - 1
        misc_s[...] = jnp.concatenate(
            [bias[...]] + grads + [jnp.zeros((spare, channels), F32)], axis=0
        ).astype(BF16)
        for step in range(1, n_lon):
            remote(misc_s, misc_r.at[lon], mp_send, mp_recv, (lat, hop(step))).start()
        misc_r[lon] = misc_s[...]

    with scope("rswait"):
        drain(rs_r.at[pl.ds(0, n_lon - 1)], rs_recv)
    with scope("zsend"):
        rs_r[lon] = tot_b[lon]
        part = rs_r[0].astype(F32)
        for p in range(1, n_lon):
            part = part + rs_r[p].astype(F32)
        z_s[...] = part.astype(BF16)
        for step in range(1, n_lat):
            remote(z_s, z_r.at[lat], z_send, z_recv, (lax.rem(lat + step, n_lat), lon)).start()
        z_r[lat] = z_s[...]
        for turn in range(1, split):
            for step in range(first_part, n_lon):
                send_strip(side(turn), step)
        for step in range(1, n_lon):
            send_strip(group, step)
        main_o[group * n_lon + lon] = con_s[group, lon]

    with scope("miscz"):
        drain(misc_r.at[pl.ds(0, n_lon - 1)], mp_recv)
        part = misc_r[0].astype(F32)
        for p in range(1, n_lon):
            part = part + misc_r[p].astype(F32)
        misc_z[...] = part.astype(BF16)
        for step in range(1, n_lat):
            remote(misc_z, misc_o.at[lat], mz_send, mz_recv, (lax.rem(lat + step, n_lat), lon)).start()
        misc_o[lat] = misc_z[...]

    with scope("zwait"):
        drain(z_r.at[pl.ds(0, n_lat - 1)], z_recv)
    with scope("agsend"):
        part = z_r[0].astype(F32)
        for p in range(1, n_lat):
            part = part + z_r[p].astype(F32)
        fin_s[...] = part.astype(BF16)
        for step in range(1, n_lon):
            remote(fin_s, sums_o.at[lon], ag_send, ag_recv, (lat, hop(step))).start()
        sums_o[lon] = fin_s[...]

    with scope("mzwait"):
        drain(misc_o.at[pl.ds(0, n_lat - 1)], mz_recv)
    with scope("conwait"):
        drain(main_o.at[pl.ds(0, holders - 1)], con_recv)

        @pl.when(has_top)
        def _():
            drain(top_o, rim_recv.at[1])

        @pl.when(has_bot)
        def _():
            drain(bot_o, rim_recv.at[0])
    with scope("agwait"):
        drain(sums_o.at[pl.ds(0, n_lon - 1)], ag_recv)

    with scope("final"):
        drain(sbuf.at[pl.ds(0, peers - 1)], row_send)
        drain(cot_r.at[pl.ds(0, holders - 1)], cot_send)

        @pl.when(jnp.logical_and(lon == n_lon - 1, lat < n_lat - 1))
        def _():
            drain(top_o, edge_send)

        @pl.when(jnp.logical_and(lon == 0, lat > 0))
        def _():
            drain(top_o, edge_send)

        drain(main_o.at[pl.ds(0, holders - 1)], con_send)
        for h in range(split):
            @pl.when(tile_lat(h) > 0)
            def _():
                drain(con_e.at[0, 0], rim_send)

            @pl.when(tile_lat(h) < n_lat - 1)
            def _():
                drain(con_e.at[0, 0], rim_send)
        drain(rs_r.at[pl.ds(0, n_lon - 1)], rs_send)
        drain(misc_r.at[pl.ds(0, n_lon - 1)], mp_send)
        drain(z_r.at[pl.ds(0, n_lat - 1)], z_send)
        drain(misc_o.at[pl.ds(0, n_lat - 1)], mz_send)
        drain(sums_o.at[pl.ds(0, n_lon - 1)], ag_send)


def finish(
    n_lat, n_lon, split, own_rows, tile_cols, taps, hidden_size,
    main, top, bot, sums, misc, grid_o, gin_o, gb_o, gout_o, gk_o,
):
    piece, channels = sums.shape[1], sums.shape[2]
    here = iota((tile_cols, channels), 0)
    bodies = []
    for j in range(n_lon):
        value = main[j].astype(F32)
        for g in range(1, split):
            value = value + main[g * n_lon + j].astype(F32)
        ends = value[own_rows * tile_cols:own_rows * tile_cols + EDGE]
        rows = []
        for y in range(own_rows):
            body = value[y * tile_cols:(y + 1) * tile_cols]
            right = ends[(EDGE - 2 * y) % EDGE:(EDGE - 2 * y) % EDGE + 1]
            left = ends[EDGE - 1 - 2 * y:EDGE - 2 * y]
            for y_at, source in ((0, top), (own_rows - 1, bot)):
                if y == y_at:
                    extra = source[j].astype(F32)
                    for g in range(1, split):
                        extra = extra + source[g * n_lon + j].astype(F32)
                    body = body + extra[0:tile_cols]
                    right = right + extra[tile_cols:tile_cols + 1]
                    left = left + extra[tile_cols + EDGE - 1:tile_cols + EDGE]
            rows.append((body, right, left))
        bodies.append(rows)
    for j in range(n_lon):
        for y in range(own_rows):
            value = bodies[j][y][0]
            value = value + jnp.where(here == 0, bodies[(j - 1) % n_lon][y][1], 0.0)
            value = value + jnp.where(here == tile_cols - 1, bodies[(j + 1) % n_lon][y][2], 0.0)
            grid_o[y, j * tile_cols:(j + 1) * tile_cols, :] = value.astype(BF16)
    for p in range(n_lon):
        value = sums[p].astype(F32)
        start = p * piece
        for ref, low, high in ((gout_o, 0, hidden_size), (gin_o, hidden_size, n_lon * piece)):
            begin, end = max(start, low), min(start + piece, high)
            if begin < end:
                ref[begin - low:end - low, :] = value[begin - start:end - start]
    value = misc[0].astype(F32)
    for z in range(1, n_lat):
        value = value + misc[z].astype(F32)
    gb_o[...] = value[0:1]
    gk_o[...] = value[1:1 + taps]


def local(
    observations, owner_device, local_cell, valid_counts,
    weight_in, bias_in, weight_out, kernel_taps, cotangent,
):
    n_lat, n_lon = lax.axis_size("lat"), lax.axis_size("lon")
    n = n_lat * n_lon
    split = split_of(n_lat)
    obs_rows, feat = observations.shape
    hidden_size, channels = weight_out.shape
    own_rows, cols, _ = cotangent.shape
    tile_rows, tile_cols = own_rows * n_lon, cols // n_lon
    cells = tile_rows * tile_cols
    slots = round_up(2 * obs_rows // n, 16)
    batch = 4 if slots > 48 else 8
    piece = (hidden_size + feat) // n_lon
    taps = kernel_taps.shape[0]
    misc_rows = round_up(taps + 1, 16)
    peers = n // split
    holders = split * n_lon
    strip_rows = own_rows * tile_cols + EDGE
    wide = tile_cols + EDGE
    scale = 1.0 / math.sqrt(obs_rows * n)
    far = functools.partial(pltpu.with_memory_space_constraint, memory_space=pltpu.HBM)
    hbm = pl.BlockSpec(memory_space=pltpu.HBM)
    vmem = pl.BlockSpec(memory_space=pltpu.VMEM)
    dma = pltpu.SemaphoreType.DMA
    V = pltpu.VMEM
    found = pl.pallas_call(
        functools.partial(kernel, n_lat, n_lon, split, slots, batch, scale),
        out_shape=(
            V((holders, strip_rows, channels), BF16),
            V((holders, wide, channels), BF16),
            V((holders, wide, channels), BF16),
            V((n_lon, piece, channels), BF16),
            V((n_lat, misc_rows, channels), BF16),
        ),
        in_specs=[hbm, hbm, hbm, pl.BlockSpec(memory_space=pltpu.SMEM)] + [hbm] * 5,
        out_specs=(vmem,) * 5,
        scratch_shapes=[
            V((obs_rows, feat), BF16), V((1, obs_rows), jnp.int32), V((obs_rows // 128, 128), jnp.int32),
            V((feat, hidden_size), BF16), V((1, hidden_size), F32), V((hidden_size, channels), BF16),
            V((taps, channels), F32), V((own_rows, cols, channels), BF16),
            V((2 * n, 128), F32), V((1, obs_rows), jnp.int32),
            V((peers, split * slots + META, feat), BF16), V((peers, split * slots + META, feat), BF16),
            V((n_lon, strip_rows, channels), BF16), V((2, n_lon, wide, channels), BF16),
            V((holders, strip_rows, channels), BF16), V((split, wide, channels), BF16), V((split, wide, channels), BF16),
            V((split, tile_rows + 2, wide, channels), F32), V((cells, channels), F32), V((split, cells, channels), BF16),
            V((split, cells, channels), F32), V((split, 3, tile_rows + 4, wide, channels), F32),
            V((split, n_lon, strip_rows, channels), BF16), V((split, 2, wide, channels), BF16),
            V((taps, 8, channels), F32), V((hidden_size + feat, channels), F32), V((1, hidden_size), F32),
            V((n_lon, piece, channels), BF16), V((n_lon, piece, channels), BF16),
            V((piece, channels), BF16), V((n_lat, piece, channels), BF16), V((piece, channels), BF16),
            V((misc_rows, channels), BF16), V((n_lon, misc_rows, channels), BF16), V((misc_rows, channels), BF16),
            dma((8,)), dma, dma((peers // batch,)), dma, dma, dma, dma((split,)), dma((split,)),
            dma, dma, dma, dma((2,)), dma, dma, dma, dma, dma, dma,
            dma, dma, dma, dma,
        ],
        compiler_params=pltpu.CompilerParams(
            collective_id=0, has_side_effects=True, vmem_limit_bytes=48 * 1024 * 1024
        ),
    )(
        far(observations), far(owner_device.reshape(1, obs_rows)), far(local_cell.reshape(obs_rows // 128, 128)),
        valid_counts, far(weight_in), far(bias_in.reshape(1, hidden_size)), far(weight_out), far(kernel_taps),
        far(cotangent),
    )
    grid_out, grad_in, grad_bias, grad_out, grad_kernel = pl.pallas_call(
        functools.partial(finish, n_lat, n_lon, split, own_rows, tile_cols, taps, hidden_size),
        out_shape=(
            jax.ShapeDtypeStruct(cotangent.shape, BF16),
            jax.ShapeDtypeStruct((feat, hidden_size), F32),
            jax.ShapeDtypeStruct((1, hidden_size), F32),
            jax.ShapeDtypeStruct((hidden_size, channels), F32),
            jax.ShapeDtypeStruct((taps, channels), F32),
        ),
        in_specs=[vmem] * 5,
        out_specs=(vmem,) * 5,
    )(*[pltpu.with_memory_space_constraint(value, pltpu.VMEM) for value in found])
    return (grid_out, grad_in, grad_bias.reshape(hidden_size), grad_out, grad_kernel)


def solution(mesh):
    return jax.shard_map(
        local,
        mesh=mesh,
        in_specs=(
            P(("lat", "lon"), None),
            P(("lat", "lon"), None),
            P(("lat", "lon")),
            P(("lat", "lon")),
            P(),
            P(),
            P(),
            P(),
            P(("lat", "lon"), None, None),
        ),
        out_specs=(P(("lat", "lon"), None, None), P(), P(), P(), P()),
        check_vma=False,
    )
```

time: 56.6 us -> 48.8 us (0.86)
  local copies, waits for them, and re-layouts: 5.51 us -> 0 us
  Pallas kernels: 49.4 us -> 47.4 us
    unnamed x13 -> x0, local copies, waits for them, and re-layouts: 4.22 us -> none
    pallas_call x1 -> x2, Pallas kernels: 49.4 us -> 47.4 us  [the longest x1 46.5 us: local(): pl.pallas_call(functools.partial(kernel, n_lat, n_lon, split, slots, batc...]
    reshape x1 -> x0, local copies, waits for them, and re-layouts: 1.3 us -> none  [local(): local_cell.reshape(1, obs_rows)]
where the time goes in v1:
time: 48.8 us; the launch traced here: 48.7 us
  Pallas kernels  47.4 us (97%)
  between operations  1.29 us (3%)
    pallas_call x1, Pallas kernels, local(): pl.pallas_call(functools.partial(kernel, n_lat, n_lon, split, slots, batc...  46.5 us

profile of v1, /device:TPU:0, one launch (start us, length us, event | category | flops | bytes accessed | tf_op | source)
XLA Modules:
  0.0 48.7 jit_solution(12847492058033995601)
XLA Ops:
  1.3 46.5 %shard_map.128 = (bf16[16,56,256]{2,1,0:T(8,128)(2,1)S(1)}, bf16[16,32,256]{2,1,0:T(8,128)(2,1)S(1)}, bf16[16,32,256]{2,1,0:T(8,128)(2,1)S(1)}, bf16[8,48,256]{2,1,0:T(8,128)(2,1)S(1)}, bf16[4,16,256]{2,1,0:T(8,128)(2,1)S(1)}) custom-call(bf16[1536,128]{1,0:T(8,128)(2,1)} %obs_h.1, s32[1,1536]{1,0:T(1,128)} %bitcast.5, s32[12,128]{1,0:T(8,128)} %bitcast.4, ...), custom_call_target="tpu_custom_call" | custom-call | tf_op jit(solution)/shard_map/pallas_call | solution.py:605
  47.8 0.9 %shard_map.129 = (bf16[2,192,256]{2,1,0:T(8,128)(2,1)}, f32[128,256]{1,0:T(8,128)}, f32[1,256]{1,0:T(1,128)}, f32[256,256]{1,0:T(8,128)}, f32[9,256]{1,0:T(8,128)}) custom-call(bf16[16,56,256]{2,1,0:T(8,128)(2,1)S(1)} %get-tuple-element.15.main, bf16[16,32,256]{2,1,0:T(8,128)(2,1)S(1)} %get-tuple-element.16.top, ...), custom_call_target="tpu_custom_call" | custom-call | tf_op jit(solution)/shard_map/pallas_call | solution.py:643

commit v2 on v1

v2 whole, which is shorter than its diff:
```python
import functools
import math

import jax
import jax.numpy as jnp
from jax import lax
from jax.experimental import pallas as pl
from jax.experimental.pallas import tpu as pltpu
from jax.sharding import PartitionSpec as P

MESH = pl.DeviceIdType.MESH
F32 = jnp.float32
BF16 = jnp.bfloat16
OFFSETS = [(a, b) for a in (-1, 0, 1) for b in (-1, 0, 1)]
CURVE = math.sqrt(2.0 / math.pi)
BEND = 0.044715
META = 8
EDGE = 8
EARLY = 2


def round_up(value, step):
    return -(-value // step) * step


def iota(shape, dim):
    return lax.broadcasted_iota(jnp.int32, shape, dim)


def dot(left, right, contract=((1,), (0,))):
    return lax.dot_general(left, right, (contract, ((), ())), preferred_element_type=F32)


def kernel(
    n_lat, n_lon, slots, batch, near_take, far_take, scale,
    obs_h, owner_h, cell_h, count, w_in_h, b_in_h, w_out_h, taps_h, cot_h,
    main_o, top_o, bot_o, sums_o, misc_o,
    obs, owner, cell, w_in, b_in, w_out, taps, cot,
    meta, slot_row, sbuf, rbuf, cot_s, cot_e, cot_r, cot_top, cot_bot, c32, adj_f, adj_b,
    dep, moved, con_s, con_e, gka, total, bias, tot_b, rs_r, z_s, z_r, fin_s, misc_s, misc_r, misc_z,
    in_sem, row_send, row_recv, cot_send, cot_recv, edge_send, top_recv, bot_recv,
    con_send, con_recv, rim_send, rim_recv, rs_send, rs_recv, z_send, z_recv, ag_send, ag_recv,
    mp_send, mp_recv, mz_send, mz_recv,
):
    n = n_lat * n_lon
    lat, lon = lax.axis_index("lat"), lax.axis_index("lon")
    me = lat * n_lon + lon
    deep = n_lat // 2
    peers = deep * n_lon
    group, level = lat // deep, lax.rem(lat, deep)
    dense = lax.rem(lon, 2) == 0
    far_lat = lax.rem(lat + deep, n_lat)
    tile_lat = (lat, far_lat)
    obs_rows, feat = obs.shape
    own_rows, cols, channels = cot.shape
    tile_rows, tile_cols = own_rows * n_lon, cols // n_lon
    cells = tile_rows * tile_cols
    wide = tile_cols + EDGE
    hidden_size = w_in.shape[1]
    piece = tot_b.shape[1]
    holders = n_lon + n_lon // 2
    scope = jax.named_scope

    def wrap(value, size):
        return jnp.where(value >= size, value - size, value)

    def hop(step):
        return wrap(lon + step, n_lon)

    def seat(off):
        return wrap(level + lax.rem(off, deep), deep), wrap(lon + off // deep, n_lon)

    def near(off):
        to_level, to_lon = seat(off)
        to_lat = group * deep + to_level
        return (to_lat, to_lon), to_lat * n_lon + to_lon

    def far(off):
        to_level, to_lon = seat(off)
        to_lat = (1 - group) * deep + to_level
        stand_in = lax.rem(to_lon, 2) == 0
        return (jnp.where(stand_in, group * deep + to_level, to_lat), to_lon), to_lat * n_lon + to_lon

    def remote(src, dst, send, recv, device):
        return pltpu.make_async_remote_copy(
            src_ref=src, dst_ref=dst, send_sem=send, recv_sem=recv,
            device_id=device, device_id_type=MESH,
        )

    def drain(ref, sem):
        pltpu.make_async_copy(ref, ref, sem).wait()

    pairs = [
        (owner_h, owner), (cell_h, cell), (obs_h, obs), (cot_h, cot),
        (w_in_h, w_in), (b_in_h, b_in), (w_out_h, w_out), (taps_h, taps),
    ]
    fetches = [pltpu.make_async_copy(src, dst, in_sem.at[i]) for i, (src, dst) in enumerate(pairs)]
    for fetch in fetches:
        fetch.start()

    barrier = pltpu.get_barrier_semaphore()

    def signal(to_lat, to_lon):
        pl.semaphore_signal(barrier, inc=1, device_id=(to_lat, to_lon), device_id_type=MESH)

    def greet(turn, carry):
        to_lat = wrap(lat + turn, n_lat)
        for step in range(n_lon):
            signal(to_lat, hop(step))
        return carry

    with scope("greet"):
        lax.fori_loop(1, n_lat, greet, 0)
        for step in range(1, n_lon):
            signal(lat, hop(step))

    with scope("zero"):
        for s in range(2):
            @pl.when(tile_lat[s] == 0)
            def _(s=s):
                cot_top[s] = jnp.zeros((wide, channels), BF16)

            @pl.when(tile_lat[s] == n_lat - 1)
            def _(s=s):
                cot_bot[s] = jnp.zeros((wide, channels), BF16)

        has_top = jnp.logical_and(lon == 0, lat > 0)
        has_bot = jnp.logical_and(lon == n_lon - 1, lat < n_lat - 1)

        @pl.when(jnp.logical_not(has_top))
        def _():
            top_o[...] = jnp.zeros_like(top_o)

        @pl.when(jnp.logical_not(has_bot))
        def _():
            bot_o[...] = jnp.zeros_like(bot_o)

    with scope("meta"):
        fetches[0].wait()
        own_row = owner[...]
        match = (own_row == iota((n, obs_rows), 0)).astype(F32)
        block = 256 if obs_rows % 256 == 0 else 128
        upper = (iota((block, block), 0) < iota((block, block), 1)).astype(F32).astype(BF16)
        carry = jnp.zeros((n, 1), F32)
        ranks = []
        for start in range(0, obs_rows, block):
            part = match[:, start:start + block]
            before = dot(part.astype(BF16), upper) + carry
            ranks.append(jnp.sum(before * part, axis=0, keepdims=True))
            carry = carry + jnp.sum(part, axis=1, keepdims=True)
        rank = jnp.concatenate(ranks, axis=1).astype(jnp.int32)
        slot_row[...] = own_row * slots + rank
        fetches[1].wait()
        lane = iota((1, obs_rows), 1)
        cells_row = jnp.concatenate([cell[i:i + 1, :] for i in range(obs_rows // 128)], axis=1)
        code = jnp.where(lane < count[0], cells_row + 1, 0)
        high = (code // 128).astype(F32)
        low = lax.rem(code, 128).astype(F32)
        coded = jnp.concatenate([match * high, match * low], axis=0).astype(BF16)
        by_rank = (rank == iota((128, obs_rows), 0)).astype(F32).astype(BF16)
        meta[...] = dot(coded, by_rank, ((1,), (1,)))
        fetches[2].wait()

    def prepare(first, where):
        base = 0 if where is near else peers
        ids = slot_row[...]
        picks = []
        targets = []
        for u in range(batch):
            _, target = where(first + u)
            targets.append(target)
            rel = jnp.clip(ids - target * slots, -1, slots).astype(F32)
            rel = jnp.broadcast_to(rel, (16, obs_rows)).astype(BF16)
            for at in range(0, slots, 16):
                line = (iota((16, obs_rows), 0) + at).astype(F32).astype(BF16)
                picks.append(jnp.where(rel == line, jnp.ones_like(line), jnp.zeros_like(line)))
        rows = dot(jnp.concatenate(picks, axis=0), obs[...]).astype(BF16)
        line = iota((META, 128), 0)
        for u in range(batch):
            at = base + first + u
            sbuf[at, 0:slots, :] = rows[u * slots:(u + 1) * slots]
            tail = jnp.where(
                line == 0, meta[pl.ds(targets[u], 1), :],
                jnp.where(line == 1, meta[pl.ds(n + targets[u], 1), :], 0.0),
            )
            sbuf[at, slots:slots + META, :] = tail.astype(BF16)

    near_takes, far_takes = peers // near_take, peers // far_take

    def ship_near(off):
        to, _ = near(off)
        remote(sbuf.at[off], rbuf.at[off], row_send, row_recv.at[off // near_take], to).start()

    def ship_far(off):
        to, _ = far(off)
        remote(
            sbuf.at[peers + off], rbuf.at[peers + off], row_send, row_recv.at[near_takes + off // far_take], to
        ).start()

    def prepare_near(p, carry):
        prepare(p * batch, near)
        return carry

    def prepare_far(p, carry):
        prepare(p * batch, far)
        return carry

    rounds = peers // batch
    with scope("prep0"):
        lax.fori_loop(0, min(EARLY, rounds), prepare_near, 0)

    with scope("cotprep"):
        fetches[3].wait()
        rim = iota((EDGE, channels), 0)
        rows_f = [cot[y].astype(F32) for y in range(own_rows)]
        for j in range(n_lon):
            start, stop = j * tile_cols, (j + 1) * tile_cols
            after, ahead = stop % cols, (start - EDGE) % cols
            mixed = jnp.zeros((EDGE, channels), F32)
            for y in range(own_rows):
                row = rows_f[y]
                ends = jnp.where(
                    rim == 0, row[after:after + EDGE],
                    jnp.where(rim == EDGE - 1, row[ahead:ahead + EDGE], 0.0),
                )
                cot_s[j, y * tile_cols:(y + 1) * tile_cols, :] = cot[y, start:stop, :]
                mixed = mixed + (pltpu.roll(ends, EDGE - 2 * y, 0) if y else ends)
                if y == 0:
                    cot_e[0, j, 0:tile_cols, :] = cot[y, start:stop, :]
                    cot_e[0, j, tile_cols:wide, :] = ends.astype(BF16)
                if y == own_rows - 1:
                    cot_e[1, j, 0:tile_cols, :] = cot[y, start:stop, :]
                    cot_e[1, j, tile_cols:wide, :] = ends.astype(BF16)
            cot_s[j, own_rows * tile_cols:own_rows * tile_cols + EDGE, :] = mixed.astype(BF16)

    with scope("barw"):
        pl.semaphore_wait(barrier, n - 1)

    with scope("ship"):
        def send_edges(e, to_tile, dst, sem):
            far_tile = lax.rem(to_tile + deep, n_lat)
            for j in range(n_lon):
                remote(cot_e.at[e, j], dst.at[0], edge_send, sem.at[0], (to_tile, j)).start()
                if j % 2 == 0:
                    remote(cot_e.at[e, j], dst.at[1], edge_send, sem.at[1], (far_tile, j)).start()

        @pl.when(jnp.logical_and(lon == n_lon - 1, lat < n_lat - 1))
        def _():
            send_edges(1, lat + 1, cot_top, top_recv)

        @pl.when(jnp.logical_and(lon == 0, lat > 0))
        def _():
            send_edges(0, lat - 1, cot_bot, bot_recv)

        for step in range(1, n_lon):
            remote(cot_s.at[hop(step)], cot_r.at[lon], cot_send, cot_recv.at[0], (lat, hop(step))).start()
        cot_r[lon] = cot_s[lon]
        for step in range(n_lon // 2):
            other = 2 * wrap(lon // 2 + step, n_lon // 2)
            remote(
                cot_s.at[other], cot_r.at[n_lon + lon], cot_send, cot_recv.at[1], (far_lat, other)
            ).start()


        def ship_first(p):
            @pl.when(p == 0)
            def _():
                pltpu.make_async_copy(sbuf.at[0], rbuf.at[0], row_recv.at[0]).start()

            @pl.when(p > 0)
            def _():
                ship_near(p * batch)

        def ship_near_batch(p, carry):
            ship_first(p)
            for u in range(1, batch):
                ship_near(p * batch + u)
            return carry

        lax.fori_loop(0, min(EARLY, rounds), ship_near_batch, 0)

    with scope("prep1"):
        if EARLY < rounds:
            lax.fori_loop(EARLY, rounds, lambda p, c: ship_near_batch(p, prepare_near(p, c)), 0)

    with scope("prep2"):
        def far_round(p, carry):
            prepare_far(p, carry)
            own = jnp.logical_and(p == 0, dense)

            @pl.when(own)
            def _():
                pltpu.make_async_copy(sbuf.at[peers], rbuf.at[peers], row_recv.at[near_takes]).start()

            @pl.when(jnp.logical_not(own))
            def _():
                ship_far(p * batch)

            for u in range(1, batch):
                ship_far(p * batch + u)
            return carry

        lax.fori_loop(0, rounds, far_round, 0)

    with scope("clear"):
        for s in range(2):
            for b in range(3):
                for i in (0, 1, tile_rows + 2, tile_rows + 3):
                    moved[s, b, i] = jnp.zeros((wide, channels), F32)
        dep[...] = jnp.zeros_like(dep)
        total[...] = jnp.zeros_like(total)
        bias[...] = jnp.zeros_like(bias)
        gka[...] = jnp.zeros_like(gka)

    def cot_wait(s):
        if s == 0:
            drain(cot_r.at[pl.ds(0, n_lon - 1)], cot_recv.at[0])
        else:
            drain(cot_r.at[pl.ds(0, n_lon)], cot_recv.at[1])

        @pl.when(tile_lat[s] > 0)
        def _():
            drain(cot_top.at[s], top_recv.at[s])

        @pl.when(tile_lat[s] < n_lat - 1)
        def _():
            drain(cot_bot.at[s], bot_recv.at[s])

    half = channels // 2
    for fetch in fetches[4:]:
        fetch.wait()
    tap = taps[...]

    def adjoint(h):
        c32[h, 0] = cot_top[h].astype(F32)
        c32[h, tile_rows + 1] = cot_bot[h].astype(F32)

        def widen(j, carry):
            at = h * n_lon + j
            ends = cot_r[at, own_rows * tile_cols:own_rows * tile_cols + EDGE, :].astype(F32)
            for r in range(own_rows):
                m = j * own_rows + r + 1
                c32[h, m, 0:tile_cols, :] = cot_r[at, r * tile_cols:(r + 1) * tile_cols, :].astype(F32)
                c32[h, m, tile_cols:wide, :] = pltpu.roll(ends, 2 * r, 0) if r else ends
            return carry

        lax.fori_loop(0, n_lon, widen, 0)

        def adjoin(m, carry):
            for c in range(0, channels, half):
                acc = jnp.zeros((tile_cols, half), F32)
                for a in (-1, 0, 1):
                    row = c32[h, m + 1 - a, :, c:c + half]
                    for b in (-1, 0, 1):
                        k = 3 * (a + 1) + b + 1
                        turned = pltpu.roll(row, b % wide, 0) if b else row
                        acc = acc + tap[k:k + 1, c:c + half] * turned[0:tile_cols]
                adj_f[pl.ds(pl.multiple_of(m * tile_cols, 8), tile_cols), c:c + half] = scale * acc
            return carry

        lax.fori_loop(0, tile_rows, adjoin, 0)
        adj_b[h] = adj_f[...].astype(BF16)

    def take(s, first, size, sem):
        with scope("rowwait"):
            drain(rbuf.at[pl.ds(first, size)], sem)
        rows = jnp.concatenate([rbuf[first + q, 0:slots, :] for q in range(size)], axis=0)
        codes = []
        for q in range(size):
            tail = rbuf[first + q, slots:slots + META, :].astype(F32)
            codes.append((128.0 * tail[0:1] + tail[1:2])[:, 0:slots])
        codes = jnp.concatenate(codes, axis=1).astype(jnp.int32)
        pick = (codes == iota((cells, size * slots), 0) + 1).astype(F32).astype(BF16)
        upstream = dot(pick, adj_b[s], ((0,), (0,))).astype(BF16)
        x = dot(rows, w_in[...]) + b_in[...]
        square = x * x
        t_val = jnp.tanh(x * (CURVE + (CURVE * BEND) * square))
        upper_half = 0.5 + 0.5 * t_val
        lower_half = 0.5 - 0.5 * t_val
        active = x * upper_half
        hidden = active.astype(BF16)
        slope = upper_half + (active * lower_half) * (2.0 * CURVE + (6.0 * CURVE * BEND) * square)
        encoded = dot(hidden, w_out[...]).astype(BF16)
        dep[s] += dot(pick, encoded)
        back = dot(upstream, w_out[...], ((1,), (1,)))
        pre = (back * slope).astype(BF16)
        total[0:hidden_size, :] += dot(hidden, upstream, ((0,), (0,)))
        total[hidden_size:hidden_size + feat, :] += dot(rows, pre, ((0,), (0,)))
        bias[...] += jnp.sum(pre.astype(F32), axis=0, keepdims=True)

    with scope("cotwaitA"):
        cot_wait(0)
    with scope("adjointA"):
        adjoint(0)

    def take_near(t, carry):
        take(0, t * near_take, near_take, row_recv.at[t])
        return carry

    def take_far(t, carry):
        take(1, peers + t * far_take, far_take, row_recv.at[near_takes + t])
        return carry

    def take_pair(t, carry):
        take_near(t + lead, carry)
        take_far(t, carry)
        return carry

    lead = rounds // 2
    with scope("takeA"):
        lax.fori_loop(0, lead, take_near, 0)
    with scope("adjointB"):
        @pl.when(dense)
        def _():
            with scope("cotwaitB"):
                cot_wait(1)
            adjoint(1)

        @pl.when(jnp.logical_not(dense))
        def _():
            adj_b[1] = adj_b[0]

    with scope("takeAB"):
        lax.fori_loop(0, rounds - lead, take_pair, 0)
    with scope("takeB"):
        lax.fori_loop(rounds - lead, rounds, take_far, 0)

    with scope("rssend"):
        for p in range(n_lon):
            tot_b[p] = total[p * piece:(p + 1) * piece, :].astype(BF16)
        for step in range(1, n_lon):
            remote(tot_b.at[hop(step)], rs_r.at[lon], rs_send, rs_recv, (lat, hop(step))).start()

    def spread(h):
        def turn_row(m, carry):
            row = dep[h, pl.ds(pl.multiple_of(m * tile_cols, 8), tile_cols), :]
            row = jnp.concatenate([row, jnp.zeros((EDGE, channels), F32)], axis=0)
            moved[h, 0, m + 2] = pltpu.roll(row, 1, 0)
            moved[h, 1, m + 2] = row
            moved[h, 2, m + 2] = pltpu.roll(row, wide - 1, 0)
            return carry

        lax.fori_loop(0, tile_rows, turn_row, 0)

        def out_row(i, c):
            acc = jnp.zeros((wide, half), F32)
            seen = c32[h, i, :, c:c + half]
            for a in (-1, 0, 1):
                for b in (-1, 0, 1):
                    k = 3 * (a + 1) + b + 1
                    value = moved[h, b + 1, i + 1 + a, :, c:c + half]
                    acc = acc + tap[k:k + 1, c:c + half] * value
                    prod = seen * value
                    folded = prod[0:8]
                    for at in range(8, wide, 8):
                        folded = folded + prod[at:at + 8]
                    gka[k, :, c:c + half] += folded
            return acc

        def strip(j, carry):
            for c in range(0, channels, half):
                mixed = jnp.zeros((EDGE, half), F32)
                for r in range(own_rows):
                    acc = out_row(j * own_rows + r + 1, c)
                    con_s[h, j, r * tile_cols:(r + 1) * tile_cols, c:c + half] = acc[0:tile_cols].astype(BF16)
                    ends = acc[tile_cols:wide]
                    mixed = mixed + (pltpu.roll(ends, EDGE - 2 * r, 0) if r else ends)
                con_s[h, j, own_rows * tile_cols:own_rows * tile_cols + EDGE, c:c + half] = mixed.astype(BF16)
            return carry

        for e, i in ((0, 0), (1, tile_rows + 1)):
            for c in range(0, channels, half):
                con_e[h, e, :, c:c + half] = out_row(i, c).astype(BF16)
        lax.fori_loop(0, n_lon, strip, 0)

    def send_strip(h, step):
        where = lon if h == 0 else n_lon + lon // 2
        remote(
            con_s.at[h, hop(step)], main_o.at[where], con_send, con_recv, (tile_lat[h], hop(step))
        ).start()

    def rim_copy(h, e):
        where = lon if h == 0 else n_lon + lon // 2
        if e == 0:
            return remote(con_e.at[h, 0], bot_o.at[where], rim_send, rim_recv.at[0], (tile_lat[h] - 1, n_lon - 1))
        return remote(con_e.at[h, 1], top_o.at[where], rim_send, rim_recv.at[1], (tile_lat[h] + 1, 0))

    def rims(h, act):
        @pl.when(tile_lat[h] > 0)
        def _():
            act(rim_copy(h, 0))

        @pl.when(tile_lat[h] < n_lat - 1)
        def _():
            act(rim_copy(h, 1))

    first_part = n_lon // 2
    with scope("spread"):
        @pl.when(dense)
        def _():
            spread(1)
            rims(1, lambda copy: copy.start())
            for step in range(first_part):
                send_strip(1, step)

        @pl.when(jnp.logical_not(dense))
        def _():
            dep[0] += dep[1]

        spread(0)
        rims(0, lambda copy: copy.start())

    with scope("misc"):
        grads = [jnp.sum(gka[k], axis=0, keepdims=True) * scale for k in range(len(OFFSETS))]
        spare = misc_s.shape[0] - len(OFFSETS) - 1
        misc_s[...] = jnp.concatenate(
            [bias[...]] + grads + [jnp.zeros((spare, channels), F32)], axis=0
        ).astype(BF16)
        for step in range(1, n_lon):
            remote(misc_s, misc_r.at[lon], mp_send, mp_recv, (lat, hop(step))).start()
        misc_r[lon] = misc_s[...]

    with scope("rswait"):
        drain(rs_r.at[pl.ds(0, n_lon - 1)], rs_recv)
    with scope("zsend"):
        rs_r[lon] = tot_b[lon]
        part = rs_r[0].astype(F32)
        for p in range(1, n_lon):
            part = part + rs_r[p].astype(F32)
        z_s[...] = part.astype(BF16)
        for step in range(1, n_lat):
            remote(z_s, z_r.at[lat], z_send, z_recv, (wrap(lat + step, n_lat), lon)).start()
        z_r[lat] = z_s[...]

        @pl.when(dense)
        def _():
            for step in range(first_part, n_lon):
                send_strip(1, step)

        for step in range(1, n_lon):
            send_strip(0, step)
        main_o[lon] = con_s[0, lon]

    with scope("miscz"):
        drain(misc_r.at[pl.ds(0, n_lon - 1)], mp_recv)
        part = misc_r[0].astype(F32)
        for p in range(1, n_lon):
            part = part + misc_r[p].astype(F32)
        misc_z[...] = part.astype(BF16)
        for step in range(1, n_lat):
            remote(misc_z, misc_o.at[lat], mz_send, mz_recv, (wrap(lat + step, n_lat), lon)).start()
        misc_o[lat] = misc_z[...]

    with scope("zwait"):
        drain(z_r.at[pl.ds(0, n_lat - 1)], z_recv)
    with scope("agsend"):
        part = z_r[0].astype(F32)
        for p in range(1, n_lat):
            part = part + z_r[p].astype(F32)
        fin_s[...] = part.astype(BF16)
        for step in range(1, n_lon):
            remote(fin_s, sums_o.at[lon], ag_send, ag_recv, (lat, hop(step))).start()
        sums_o[lon] = fin_s[...]

    with scope("mzwait"):
        drain(misc_o.at[pl.ds(0, n_lat - 1)], mz_recv)
    with scope("conwait"):
        drain(main_o.at[pl.ds(0, holders - 1)], con_recv)

        @pl.when(has_top)
        def _():
            drain(top_o, rim_recv.at[1])

        @pl.when(has_bot)
        def _():
            drain(bot_o, rim_recv.at[0])
    with scope("agwait"):
        drain(sums_o.at[pl.ds(0, n_lon - 1)], ag_recv)

    with scope("final"):
        drain(sbuf.at[pl.ds(0, 2 * peers - 2)], row_send)

        @pl.when(jnp.logical_not(dense))
        def _():
            drain(sbuf.at[0], row_send)

        drain(cot_r.at[pl.ds(0, holders - 1)], cot_send)

        @pl.when(jnp.logical_and(lon == n_lon - 1, lat < n_lat - 1))
        def _():
            drain(top_o, edge_send)

        @pl.when(jnp.logical_and(lon == 0, lat > 0))
        def _():
            drain(top_o, edge_send)

        drain(main_o.at[pl.ds(0, n_lon - 1)], con_send)
        rims(0, lambda copy: copy.wait_send())

        @pl.when(dense)
        def _():
            drain(main_o.at[pl.ds(0, n_lon)], con_send)
            rims(1, lambda copy: copy.wait_send())

        drain(rs_r.at[pl.ds(0, n_lon - 1)], rs_send)
        drain(misc_r.at[pl.ds(0, n_lon - 1)], mp_send)
        drain(z_r.at[pl.ds(0, n_lat - 1)], z_send)
        drain(misc_o.at[pl.ds(0, n_lat - 1)], mz_send)
        drain(sums_o.at[pl.ds(0, n_lon - 1)], ag_send)


def finish(
    n_lat, n_lon, own_rows, tile_cols, taps, hidden_size,
    main, top, bot, sums, misc, grid_o, gin_o, gb_o, gout_o, gk_o,
):
    piece, channels = sums.shape[1], sums.shape[2]
    here = iota((tile_cols, channels), 0)

    def both(ref, j):
        value = ref[j].astype(F32)
        return value if j % 2 else value + ref[n_lon + j // 2].astype(F32)

    bodies = []
    for j in range(n_lon):
        value = both(main, j)
        ends = value[own_rows * tile_cols:own_rows * tile_cols + EDGE]
        rows = []
        for y in range(own_rows):
            body = value[y * tile_cols:(y + 1) * tile_cols]
            right = ends[(EDGE - 2 * y) % EDGE:(EDGE - 2 * y) % EDGE + 1]
            left = ends[EDGE - 1 - 2 * y:EDGE - 2 * y]
            for y_at, source in ((0, top), (own_rows - 1, bot)):
                if y == y_at:
                    extra = both(source, j)
                    body = body + extra[0:tile_cols]
                    right = right + extra[tile_cols:tile_cols + 1]
                    left = left + extra[tile_cols + EDGE - 1:tile_cols + EDGE]
            rows.append((body, right, left))
        bodies.append(rows)
    for j in range(n_lon):
        for y in range(own_rows):
            value = bodies[j][y][0]
            value = value + jnp.where(here == 0, bodies[(j - 1) % n_lon][y][1], 0.0)
            value = value + jnp.where(here == tile_cols - 1, bodies[(j + 1) % n_lon][y][2], 0.0)
            grid_o[y, j * tile_cols:(j + 1) * tile_cols, :] = value.astype(BF16)
    for p in range(n_lon):
        value = sums[p].astype(F32)
        start = p * piece
        for ref, low, high in ((gout_o, 0, hidden_size), (gin_o, hidden_size, n_lon * piece)):
            begin, end = max(start, low), min(start + piece, high)
            if begin < end:
                ref[begin - low:end - low, :] = value[begin - start:end - start]
    value = misc[0].astype(F32)
    for z in range(1, n_lat):
        value = value + misc[z].astype(F32)
    gb_o[...] = value[0:1]
    gk_o[...] = value[1:1 + taps]


def local(
    observations, owner_device, local_cell, valid_counts,
    weight_in, bias_in, weight_out, kernel_taps, cotangent,
):
    n_lat, n_lon = lax.axis_size("lat"), lax.axis_size("lon")
    n = n_lat * n_lon
    obs_rows, feat = observations.shape
    hidden_size, channels = weight_out.shape
    own_rows, cols, _ = cotangent.shape
    tile_rows, tile_cols = own_rows * n_lon, cols // n_lon
    cells = tile_rows * tile_cols
    slots = round_up(2 * obs_rows // n, 16)
    batch = 4 if slots > 48 else 8
    near_take, far_take = batch, batch
    piece = (hidden_size + feat) // n_lon
    taps = kernel_taps.shape[0]
    misc_rows = round_up(taps + 1, 16)
    peers = n // 2
    holders = n_lon + n_lon // 2
    strip_rows = own_rows * tile_cols + EDGE
    wide = tile_cols + EDGE
    scale = 1.0 / math.sqrt(obs_rows * n)
    far = functools.partial(pltpu.with_memory_space_constraint, memory_space=pltpu.HBM)
    hbm = pl.BlockSpec(memory_space=pltpu.HBM)
    vmem = pl.BlockSpec(memory_space=pltpu.VMEM)
    dma = pltpu.SemaphoreType.DMA
    V = pltpu.VMEM
    found = pl.pallas_call(
        functools.partial(kernel, n_lat, n_lon, slots, batch, near_take, far_take, scale),
        out_shape=(
            V((holders, strip_rows, channels), BF16),
            V((holders, wide, channels), BF16),
            V((holders, wide, channels), BF16),
            V((n_lon, piece, channels), BF16),
            V((n_lat, misc_rows, channels), BF16),
        ),
        in_specs=[hbm, hbm, hbm, pl.BlockSpec(memory_space=pltpu.SMEM)] + [hbm] * 5,
        out_specs=(vmem,) * 5,
        scratch_shapes=[
            V((obs_rows, feat), BF16), V((1, obs_rows), jnp.int32), V((obs_rows // 128, 128), jnp.int32),
            V((feat, hidden_size), BF16), V((1, hidden_size), F32), V((hidden_size, channels), BF16),
            V((taps, channels), F32), V((own_rows, cols, channels), BF16),
            V((2 * n, 128), F32), V((1, obs_rows), jnp.int32),
            V((n, slots + META, feat), BF16), V((n, slots + META, feat), BF16),
            V((n_lon, strip_rows, channels), BF16), V((2, n_lon, wide, channels), BF16),
            V((2 * n_lon, strip_rows, channels), BF16), V((2, wide, channels), BF16), V((2, wide, channels), BF16),
            V((2, tile_rows + 2, wide, channels), F32), V((cells, channels), F32), V((2, cells, channels), BF16),
            V((2, cells, channels), F32), V((2, 3, tile_rows + 4, wide, channels), F32),
            V((2, n_lon, strip_rows, channels), BF16), V((2, 2, wide, channels), BF16),
            V((taps, 8, channels), F32), V((hidden_size + feat, channels), F32), V((1, hidden_size), F32),
            V((n_lon, piece, channels), BF16), V((n_lon, piece, channels), BF16),
            V((piece, channels), BF16), V((n_lat, piece, channels), BF16), V((piece, channels), BF16),
            V((misc_rows, channels), BF16), V((n_lon, misc_rows, channels), BF16), V((misc_rows, channels), BF16),
            dma((8,)), dma, dma((peers // near_take + peers // far_take,)), dma, dma((2,)), dma, dma((2,)), dma((2,)),
            dma, dma, dma, dma((2,)), dma, dma, dma, dma, dma, dma,
            dma, dma, dma, dma,
        ],
        compiler_params=pltpu.CompilerParams(
            collective_id=0, has_side_effects=True, vmem_limit_bytes=48 * 1024 * 1024
        ),
    )(
        far(observations), far(owner_device.reshape(1, obs_rows)), far(local_cell.reshape(obs_rows // 128, 128)),
        valid_counts, far(weight_in), far(bias_in.reshape(1, hidden_size)), far(weight_out), far(kernel_taps),
        far(cotangent),
    )
    grid_out, grad_in, grad_bias, grad_out, grad_kernel = pl.pallas_call(
        functools.partial(finish, n_lat, n_lon, own_rows, tile_cols, taps, hidden_size),
        out_shape=(
            jax.ShapeDtypeStruct(cotangent.shape, BF16),
            jax.ShapeDtypeStruct((feat, hidden_size), F32),
            jax.ShapeDtypeStruct((1, hidden_size), F32),
            jax.ShapeDtypeStruct((hidden_size, channels), F32),
            jax.ShapeDtypeStruct((taps, channels), F32),
        ),
        in_specs=[vmem] * 5,
        out_specs=(vmem,) * 5,
    )(*[pltpu.with_memory_space_constraint(value, pltpu.VMEM) for value in found])
    return (grid_out, grad_in, grad_bias.reshape(hidden_size), grad_out, grad_kernel)


def solution(mesh):
    return jax.shard_map(
        local,
        mesh=mesh,
        in_specs=(
            P(("lat", "lon"), None),
            P(("lat", "lon"), None),
            P(("lat", "lon")),
            P(("lat", "lon")),
            P(),
            P(),
            P(),
            P(),
            P(("lat", "lon"), None, None),
        ),
        out_specs=(P(("lat", "lon"), None, None), P(), P(), P(), P()),
        check_vma=False,
    )
```

time: 48.8 us -> 41.5 us (0.85)
  Pallas kernels: 47.4 us -> 40 us
    pallas_call x2, Pallas kernels: 47.4 us -> 40 us  [the longest x1 39.1 us: local(): pl.pallas_call(functools.partial(kernel, n_lat, n_lon, slots, batch, near...]
where the time goes in v2:
time: 41.5 us; the launch traced here: 41.3 us
  Pallas kernels  40 us (96%)
  between operations  1.29 us (3%)
    pallas_call x1, Pallas kernels, local(): pl.pallas_call(functools.partial(kernel, n_lat, n_lon, slots, batch, near...  39.1 us
    pallas_call x1, Pallas kernels, local(): pl.pallas_call(functools.partial(finish, n_lat, n_lon, own_rows, tile_col...  0.85 us

profile of v2, /device:TPU:0, one launch (start us, length us, event | category | flops | bytes accessed | tf_op | source)
XLA Modules:
  0.0 41.3 jit_solution(9098836423413089626)
XLA Ops:
  1.3 39.1 %shard_map.128 = (bf16[12,56,256]{2,1,0:T(8,128)(2,1)S(1)}, bf16[12,32,256]{2,1,0:T(8,128)(2,1)S(1)}, bf16[12,32,256]{2,1,0:T(8,128)(2,1)S(1)}, bf16[8,48,256]{2,1,0:T(8,128)(2,1)S(1)}, bf16[4,16,256]{2,1,0:T(8,128)(2,1)S(1)}) custom-call(bf16[1536,128]{1,0:T(8,128)(2,1)} %obs_h.1, s32[1,1536]{1,0:T(1,128)} %bitcast.5, s32[12,128]{1,0:T(8,128)} %bitcast.4, ...), custom_call_target="tpu_custom_call" | custom-call | tf_op jit(solution)/shard_map/pallas_call | solution.py:687
  40.4 0.9 %shard_map.129 = (bf16[2,192,256]{2,1,0:T(8,128)(2,1)}, f32[128,256]{1,0:T(8,128)}, f32[1,256]{1,0:T(1,128)}, f32[256,256]{1,0:T(8,128)}, f32[9,256]{1,0:T(8,128)}) custom-call(bf16[12,56,256]{2,1,0:T(8,128)(2,1)S(1)} %get-tuple-element.15.main, bf16[12,32,256]{2,1,0:T(8,128)(2,1)S(1)} %get-tuple-element.16.top, ...), custom_call_target="tpu_custom_call" | custom-call | tf_op jit(solution)/shard_map/pallas_call | solution.py:725

commit v3 on v2

--- a/solution.py
+++ b/solution.py
@@ -14,9 +14,10 @@
 OFFSETS = [(a, b) for a in (-1, 0, 1) for b in (-1, 0, 1)]
 CURVE = math.sqrt(2.0 / math.pi)
 BEND = 0.044715
-META = 8
 EDGE = 8
 EARLY = 2
+SEND = (("n", 0), ("n", 1), ("n", 2), ("n", 3), ("f", 0), ("f", 1), ("f", 2), ("f", 3))
+LATE = 2
 
 
 def round_up(value, step):
@@ -32,13 +33,14 @@
 
 
 def kernel(
-    n_lat, n_lon, slots, batch, near_take, far_take, scale,
+    n_lat, n_lon, slots, batch, scale,
     obs_h, owner_h, cell_h, count, w_in_h, b_in_h, w_out_h, taps_h, cot_h,
+    grid_o, gin_o, gb_o, gout_o, gk_o,
+    obs, owner, cell, w_in, b_in, w_out, taps, cot,
     main_o, top_o, bot_o, sums_o, misc_o,
-    obs, owner, cell, w_in, b_in, w_out, taps, cot,
-    meta, slot_row, sbuf, rbuf, cot_s, cot_e, cot_r, cot_top, cot_bot, c32, adj_f, adj_b,
+    meta, meta_r, slot_row, sbuf, rbuf, cot_s, cot_e, cot_r, cot_top, cot_bot, c32, adj_f, adj_b,
     dep, moved, con_s, con_e, gka, total, bias, tot_b, rs_r, z_s, z_r, fin_s, misc_s, misc_r, misc_z,
-    in_sem, row_send, row_recv, cot_send, cot_recv, edge_send, top_recv, bot_recv,
+    in_sem, meta_send, meta_recv, row_send, row_recv, cot_send, cot_recv, edge_send, top_recv, bot_recv,
     con_send, con_recv, rim_send, rim_recv, rs_send, rs_recv, z_send, z_recv, ag_send, ag_recv,
     mp_send, mp_recv, mz_send, mz_recv,
 ):
@@ -68,7 +70,7 @@
         return wrap(lon + step, n_lon)
 
     def seat(off):
-        return wrap(level + lax.rem(off, deep), deep), wrap(lon + off // deep, n_lon)
+        return wrap(level + off // n_lon, deep), wrap(lon + lax.rem(off, n_lon), n_lon)
 
     def near(off):
         to_level, to_lon = seat(off)
@@ -158,7 +160,8 @@
         low = lax.rem(code, 128).astype(F32)
         coded = jnp.concatenate([match * high, match * low], axis=0).astype(BF16)
         by_rank = (rank == iota((128, obs_rows), 0)).astype(F32).astype(BF16)
-        meta[...] = dot(coded, by_rank, ((1,), (1,)))
+        parts = dot(coded, by_rank, ((1,), (1,)))
+        meta[...] = (128.0 * parts[0:n] + parts[n:2 * n]).astype(jnp.int32).reshape(n, 1, 128)
         fetches[2].wait()
 
     def prepare(first, where):
@@ -175,39 +178,69 @@
                 line = (iota((16, obs_rows), 0) + at).astype(F32).astype(BF16)
                 picks.append(jnp.where(rel == line, jnp.ones_like(line), jnp.zeros_like(line)))
         rows = dot(jnp.concatenate(picks, axis=0), obs[...]).astype(BF16)
-        line = iota((META, 128), 0)
         for u in range(batch):
-            at = base + first + u
-            sbuf[at, 0:slots, :] = rows[u * slots:(u + 1) * slots]
-            tail = jnp.where(
-                line == 0, meta[pl.ds(targets[u], 1), :],
-                jnp.where(line == 1, meta[pl.ds(n + targets[u], 1), :], 0.0),
-            )
-            sbuf[at, slots:slots + META, :] = tail.astype(BF16)
-
-    near_takes, far_takes = peers // near_take, peers // far_take
-
-    def ship_near(off):
-        to, _ = near(off)
-        remote(sbuf.at[off], rbuf.at[off], row_send, row_recv.at[off // near_take], to).start()
-
-    def ship_far(off):
-        to, _ = far(off)
-        remote(
-            sbuf.at[peers + off], rbuf.at[peers + off], row_send, row_recv.at[near_takes + off // far_take], to
-        ).start()
-
-    def prepare_near(p, carry):
-        prepare(p * batch, near)
-        return carry
-
-    def prepare_far(p, carry):
-        prepare(p * batch, far)
-        return carry
+            sbuf[base + first + u] = rows[u * slots:(u + 1) * slots]
+
+    def ship_unit(off, where, base):
+        to, target = where(off)
+        at = base + off
+        remote(meta.at[target], meta_r.at[at], meta_send, meta_recv.at[at // batch], to).start()
+        remote(sbuf.at[at], rbuf.at[at], row_send, row_recv.at[at // batch], to).start()
 
     rounds = peers // batch
+
+    def loops(order, body):
+        at = 0
+        while at < len(order):
+            kind, first = order[at]
+            last = at + 1
+            while last < len(order) and order[last] == (kind, first + last - at):
+                last += 1
+            if last - at == 1:
+                body(kind, first)
+            else:
+                def step(p, carry, kind=kind):
+                    body(kind, p)
+                    return carry
+
+                lax.fori_loop(first, first + last - at, step, 0)
+            at = last
+
+    def order_of(quarters):
+        part = rounds // 4
+        return [(kind, q * part + i) for kind, q in quarters for i in range(part)]
+
+    send_order = order_of(SEND)
+
+    def prepare_step(kind, p):
+        prepare(p * batch, near if kind == "n" else far)
+
+    def ship_step(kind, p):
+        where, base = (near, 0) if kind == "n" else (far, peers)
+        own = p == 0 if kind == "n" else jnp.logical_and(p == 0, dense)
+        if isinstance(p, int) and p > 0:
+            ship_unit(p * batch, where, base)
+        else:
+            @pl.when(own)
+            def _():
+                _, target = where(0)
+                pltpu.make_async_copy(meta.at[target], meta_r.at[base], meta_recv.at[base // batch]).start()
+                pltpu.make_async_copy(sbuf.at[base], rbuf.at[base], row_recv.at[base // batch]).start()
+
+            @pl.when(jnp.logical_not(own))
+            def _():
+                ship_unit(p * batch, where, base)
+
+        for u in range(1, batch):
+            ship_unit(p * batch + u, where, base)
+
+    def both_step(kind, p):
+        prepare_step(kind, p)
+        ship_step(kind, p)
+
+    ready = rounds // 4 * EARLY
     with scope("prep0"):
-        lax.fori_loop(0, min(EARLY, rounds), prepare_near, 0)
+        loops(send_order[:ready], prepare_step)
 
     with scope("cotprep"):
         fetches[3].wait()
@@ -237,70 +270,34 @@
         pl.semaphore_wait(barrier, n - 1)
 
     with scope("ship"):
-        def send_edges(e, to_tile, dst, sem):
-            far_tile = lax.rem(to_tile + deep, n_lat)
-            for j in range(n_lon):
-                remote(cot_e.at[e, j], dst.at[0], edge_send, sem.at[0], (to_tile, j)).start()
-                if j % 2 == 0:
-                    remote(cot_e.at[e, j], dst.at[1], edge_send, sem.at[1], (far_tile, j)).start()
-
-        @pl.when(jnp.logical_and(lon == n_lon - 1, lat < n_lat - 1))
-        def _():
-            send_edges(1, lat + 1, cot_top, top_recv)
-
-        @pl.when(jnp.logical_and(lon == 0, lat > 0))
-        def _():
-            send_edges(0, lat - 1, cot_bot, bot_recv)
+        def send_edges(far_side):
+            def go(e, to_tile, dst, sem):
+                to_lat = lax.rem(to_tile + deep, n_lat) if far_side else to_tile
+                for j in range(0, n_lon, 1 + far_side):
+                    remote(cot_e.at[e, j], dst.at[far_side], edge_send, sem.at[far_side], (to_lat, j)).start()
+
+            @pl.when(jnp.logical_and(lon == n_lon - 1, lat < n_lat - 1))
+            def _():
+                go(1, lat + 1, cot_top, top_recv)
+
+            @pl.when(jnp.logical_and(lon == 0, lat > 0))
+            def _():
+                go(0, lat - 1, cot_bot, bot_recv)
 
         for step in range(1, n_lon):
             remote(cot_s.at[hop(step)], cot_r.at[lon], cot_send, cot_recv.at[0], (lat, hop(step))).start()
         cot_r[lon] = cot_s[lon]
+        send_edges(0)
         for step in range(n_lon // 2):
             other = 2 * wrap(lon // 2 + step, n_lon // 2)
             remote(
                 cot_s.at[other], cot_r.at[n_lon + lon], cot_send, cot_recv.at[1], (far_lat, other)
             ).start()
-
-
-        def ship_first(p):
-            @pl.when(p == 0)
-            def _():
-                pltpu.make_async_copy(sbuf.at[0], rbuf.at[0], row_recv.at[0]).start()
-
-            @pl.when(p > 0)
-            def _():
-                ship_near(p * batch)
-
-        def ship_near_batch(p, carry):
-            ship_first(p)
-            for u in range(1, batch):
-                ship_near(p * batch + u)
-            return carry
-
-        lax.fori_loop(0, min(EARLY, rounds), ship_near_batch, 0)
-
-    with scope("prep1"):
-        if EARLY < rounds:
-            lax.fori_loop(EARLY, rounds, lambda p, c: ship_near_batch(p, prepare_near(p, c)), 0)
-
+        send_edges(1)
+
+        loops(send_order[:ready], ship_step)
     with scope("prep2"):
-        def far_round(p, carry):
-            prepare_far(p, carry)
-            own = jnp.logical_and(p == 0, dense)
-
-            @pl.when(own)
-            def _():
-                pltpu.make_async_copy(sbuf.at[peers], rbuf.at[peers], row_recv.at[near_takes]).start()
-
-            @pl.when(jnp.logical_not(own))
-            def _():
-                ship_far(p * batch)
-
-            for u in range(1, batch):
-                ship_far(p * batch + u)
-            return carry
-
-        lax.fori_loop(0, rounds, far_round, 0)
+        loops(send_order[ready:], both_step)
 
     with scope("clear"):
         for s in range(2):
@@ -361,15 +358,15 @@
         lax.fori_loop(0, tile_rows, adjoin, 0)
         adj_b[h] = adj_f[...].astype(BF16)
 
-    def take(s, first, size, sem):
+    def take(step, count):
+        first, size = step * batch, count * batch
+        s = first // peers
         with scope("rowwait"):
-            drain(rbuf.at[pl.ds(first, size)], sem)
-        rows = jnp.concatenate([rbuf[first + q, 0:slots, :] for q in range(size)], axis=0)
-        codes = []
-        for q in range(size):
-            tail = rbuf[first + q, slots:slots + META, :].astype(F32)
-            codes.append((128.0 * tail[0:1] + tail[1:2])[:, 0:slots])
-        codes = jnp.concatenate(codes, axis=1).astype(jnp.int32)
+            for i in range(count):
+                drain(meta_r.at[pl.ds(first + i * batch, batch)], meta_recv.at[step + i])
+                drain(rbuf.at[pl.ds(first + i * batch, batch)], row_recv.at[step + i])
+        rows = jnp.concatenate([rbuf[first + q] for q in range(size)], axis=0)
+        codes = jnp.concatenate([meta_r[first + q][:, 0:slots] for q in range(size)], axis=1)
         pick = (codes == iota((cells, size * slots), 0) + 1).astype(F32).astype(BF16)
         upstream = dot(pick, adj_b[s], ((0,), (0,))).astype(BF16)
         x = dot(rows, w_in[...]) + b_in[...]
@@ -393,22 +390,18 @@
     with scope("adjointA"):
         adjoint(0)
 
-    def take_near(t, carry):
-        take(0, t * near_take, near_take, row_recv.at[t])
+    part = rounds // 4
+
+    def take_pair(g, carry):
+        take(2 * part * g, 2 * part)
         return carry
 
-    def take_far(t, carry):
-        take(1, peers + t * far_take, far_take, row_recv.at[near_takes + t])
+    def take_one(g, carry):
+        take(part * g, part)
         return carry
 
-    def take_pair(t, carry):
-        take_near(t + lead, carry)
-        take_far(t, carry)
-        return carry
-
-    lead = rounds // 2
-    with scope("takeA"):
-        lax.fori_loop(0, lead, take_near, 0)
+    with scope("take1"):
+        lax.fori_loop(0, 1, take_pair, 0)
     with scope("adjointB"):
         @pl.when(dense)
         def _():
@@ -420,10 +413,11 @@
         def _():
             adj_b[1] = adj_b[0]
 
-    with scope("takeAB"):
-        lax.fori_loop(0, rounds - lead, take_pair, 0)
-    with scope("takeB"):
-        lax.fori_loop(rounds - lead, rounds, take_far, 0)
+    with scope("take2"):
+        lax.fori_loop(1, 4 - LATE // 2, take_pair, 0)
+    with scope("take3"):
+        if LATE:
+            lax.fori_loop(8 - LATE, 8, take_one, 0)
 
     with scope("rssend"):
         for p in range(n_lon):
@@ -574,15 +568,60 @@
         @pl.when(has_bot)
         def _():
             drain(bot_o, rim_recv.at[0])
+    with scope("grid"):
+        value = misc_o[0].astype(F32)
+        for z in range(1, n_lat):
+            value = value + misc_o[z].astype(F32)
+        gb_o[...] = value[0:1]
+        gk_o[...] = value[1:1 + len(OFFSETS)]
+        here = iota((tile_cols, channels), 0)
+
+        def both(ref, j):
+            value = ref[j].astype(F32)
+            return value if j % 2 else value + ref[n_lon + j // 2].astype(F32)
+
+        bodies = []
+        for j in range(n_lon):
+            value = both(main_o, j)
+            ends = value[own_rows * tile_cols:own_rows * tile_cols + EDGE]
+            rows = []
+            for y in range(own_rows):
+                body = value[y * tile_cols:(y + 1) * tile_cols]
+                right = ends[(EDGE - 2 * y) % EDGE:(EDGE - 2 * y) % EDGE + 1]
+                left = ends[EDGE - 1 - 2 * y:EDGE - 2 * y]
+                for y_at, source in ((0, top_o), (own_rows - 1, bot_o)):
+                    if y == y_at:
+                        extra = both(source, j)
+                        body = body + extra[0:tile_cols]
+                        right = right + extra[tile_cols:tile_cols + 1]
+                        left = left + extra[tile_cols + EDGE - 1:tile_cols + EDGE]
+                rows.append((body, right, left))
+            bodies.append(rows)
+        for j in range(n_lon):
+            for y in range(own_rows):
+                value = bodies[j][y][0]
+                value = value + jnp.where(here == 0, bodies[(j - 1) % n_lon][y][1], 0.0)
+                value = value + jnp.where(here == tile_cols - 1, bodies[(j + 1) % n_lon][y][2], 0.0)
+                grid_o[y, j * tile_cols:(j + 1) * tile_cols, :] = value.astype(BF16)
     with scope("agwait"):
         drain(sums_o.at[pl.ds(0, n_lon - 1)], ag_recv)
+    with scope("sums"):
+        for p in range(n_lon):
+            value = sums_o[p].astype(F32)
+            start = p * piece
+            for ref, low, high in ((gout_o, 0, hidden_size), (gin_o, hidden_size, n_lon * piece)):
+                begin, end = max(start, low), min(start + piece, high)
+                if begin < end:
+                    ref[begin - low:end - low, :] = value[begin - start:end - start]
 
     with scope("final"):
         drain(sbuf.at[pl.ds(0, 2 * peers - 2)], row_send)
+        drain(meta_r.at[pl.ds(0, 2 * peers - 2)], meta_send)
 
         @pl.when(jnp.logical_not(dense))
         def _():
             drain(sbuf.at[0], row_send)
+            drain(meta_r.at[0], meta_send)
 
         drain(cot_r.at[pl.ds(0, holders - 1)], cot_send)
 
@@ -609,52 +648,13 @@
         drain(sums_o.at[pl.ds(0, n_lon - 1)], ag_send)
 
 
-def finish(
-    n_lat, n_lon, own_rows, tile_cols, taps, hidden_size,
-    main, top, bot, sums, misc, grid_o, gin_o, gb_o, gout_o, gk_o,
-):
-    piece, channels = sums.shape[1], sums.shape[2]
-    here = iota((tile_cols, channels), 0)
-
-    def both(ref, j):
-        value = ref[j].astype(F32)
-        return value if j % 2 else value + ref[n_lon + j // 2].astype(F32)
-
-    bodies = []
-    for j in range(n_lon):
-        value = both(main, j)
-        ends = value[own_rows * tile_cols:own_rows * tile_cols + EDGE]
-        rows = []
-        for y in range(own_rows):
-            body = value[y * tile_cols:(y + 1) * tile_cols]
-            right = ends[(EDGE - 2 * y) % EDGE:(EDGE - 2 * y) % EDGE + 1]
-            left = ends[EDGE - 1 - 2 * y:EDGE - 2 * y]
-            for y_at, source in ((0, top), (own_rows - 1, bot)):
-                if y == y_at:
-                    extra = both(source, j)
-                    body = body + extra[0:tile_cols]
-                    right = right + extra[tile_cols:tile_cols + 1]
-                    left = left + extra[tile_cols + EDGE - 1:tile_cols + EDGE]
-            rows.append((body, right, left))
-        bodies.append(rows)
-    for j in range(n_lon):
-        for y in range(own_rows):
-            value = bodies[j][y][0]
-            value = value + jnp.where(here == 0, bodies[(j - 1) % n_lon][y][1], 0.0)
-            value = value + jnp.where(here == tile_cols - 1, bodies[(j + 1) % n_lon][y][2], 0.0)
-            grid_o[y, j * tile_cols:(j + 1) * tile_cols, :] = value.astype(BF16)
-    for p in range(n_lon):
-        value = sums[p].astype(F32)
-        start = p * piece
-        for ref, low, high in ((gout_o, 0, hidden_size), (gin_o, hidden_size, n_lon * piece)):
-            begin, end = max(start, low), min(start + piece, high)
-            if begin < end:
-                ref[begin - low:end - low, :] = value[begin - start:end - start]
-    value = misc[0].astype(F32)
-    for z in range(1, n_lat):
-        value = value + misc[z].astype(F32)
-    gb_o[...] = value[0:1]
-    gk_o[...] = value[1:1 + taps]
+def finish(*refs):
+    sem, half = refs[-1], (len(refs) - 1) // 2
+    copies = [pltpu.make_async_copy(refs[i], refs[half + i], sem.at[i]) for i in range(half)]
+    for copy in copies:
+        copy.start()
+    for copy in copies:
+        copy.wait()
 
 
 def local(
@@ -670,7 +670,6 @@
     cells = tile_rows * tile_cols
     slots = round_up(2 * obs_rows // n, 16)
     batch = 4 if slots > 48 else 8
-    near_take, far_take = batch, batch
     piece = (hidden_size + feat) // n_lon
     taps = kernel_taps.shape[0]
     misc_rows = round_up(taps + 1, 16)
@@ -679,28 +678,29 @@
     strip_rows = own_rows * tile_cols + EDGE
     wide = tile_cols + EDGE
     scale = 1.0 / math.sqrt(obs_rows * n)
+    results = (
+        (cotangent.shape, BF16), ((feat, hidden_size), F32), ((1, hidden_size), F32),
+        ((hidden_size, channels), F32), ((taps, channels), F32),
+    )
     far = functools.partial(pltpu.with_memory_space_constraint, memory_space=pltpu.HBM)
     hbm = pl.BlockSpec(memory_space=pltpu.HBM)
     vmem = pl.BlockSpec(memory_space=pltpu.VMEM)
     dma = pltpu.SemaphoreType.DMA
     V = pltpu.VMEM
     found = pl.pallas_call(
-        functools.partial(kernel, n_lat, n_lon, slots, batch, near_take, far_take, scale),
-        out_shape=(
-            V((holders, strip_rows, channels), BF16),
-            V((holders, wide, channels), BF16),
-            V((holders, wide, channels), BF16),
-            V((n_lon, piece, channels), BF16),
-            V((n_lat, misc_rows, channels), BF16),
-        ),
+        functools.partial(kernel, n_lat, n_lon, slots, batch, scale),
+        out_shape=tuple(V(shape, kind) for shape, kind in results),
         in_specs=[hbm, hbm, hbm, pl.BlockSpec(memory_space=pltpu.SMEM)] + [hbm] * 5,
         out_specs=(vmem,) * 5,
         scratch_shapes=[
             V((obs_rows, feat), BF16), V((1, obs_rows), jnp.int32), V((obs_rows // 128, 128), jnp.int32),
             V((feat, hidden_size), BF16), V((1, hidden_size), F32), V((hidden_size, channels), BF16),
             V((taps, channels), F32), V((own_rows, cols, channels), BF16),
-            V((2 * n, 128), F32), V((1, obs_rows), jnp.int32),
-            V((n, slots + META, feat), BF16), V((n, slots + META, feat), BF16),
+            V((holders, strip_rows, channels), BF16), V((holders, wide, channels), BF16),
+            V((holders, wide, channels), BF16), V((n_lon, piece, channels), BF16),
+            V((n_lat, misc_rows, channels), BF16),
+            V((n, 1, 128), jnp.int32), V((n, 1, 128), jnp.int32), V((1, obs_rows), jnp.int32),
+            V((n, slots, feat), BF16), V((n, slots, feat), BF16),
             V((n_lon, strip_rows, channels), BF16), V((2, n_lon, wide, channels), BF16),
             V((2 * n_lon, strip_rows, channels), BF16), V((2, wide, channels), BF16), V((2, wide, channels), BF16),
             V((2, tile_rows + 2, wide, channels), F32), V((cells, channels), F32), V((2, cells, channels), BF16),
@@ -710,7 +710,7 @@
             V((n_lon, piece, channels), BF16), V((n_lon, piece, channels), BF16),
             V((piece, channels), BF16), V((n_lat, piece, channels), BF16), V((piece, channels), BF16),
             V((misc_rows, channels), BF16), V((n_lon, misc_rows, channels), BF16), V((misc_rows, channels), BF16),
-            dma((8,)), dma, dma((peers // near_take + peers // far_take,)), dma, dma((2,)), dma, dma((2,)), dma((2,)),
+            dma((8,)), dma, dma((n // batch,)), dma, dma((n // batch,)), dma, dma((2,)), dma, dma((2,)), dma((2,)),
             dma, dma, dma, dma((2,)), dma, dma, dma, dma, dma, dma,
             dma, dma, dma, dma,
         ],
@@ -723,16 +723,11 @@
         far(cotangent),
     )
     grid_out, grad_in, grad_bias, grad_out, grad_kernel = pl.pallas_call(
-        functools.partial(finish, n_lat, n_lon, own_rows, tile_cols, taps, hidden_size),
-        out_shape=(
-            jax.ShapeDtypeStruct(cotangent.shape, BF16),
-            jax.ShapeDtypeStruct((feat, hidden_size), F32),
-            jax.ShapeDtypeStruct((1, hidden_size), F32),
-            jax.ShapeDtypeStruct((hidden_size, channels), F32),
-            jax.ShapeDtypeStruct((taps, channels), F32),
-        ),
+        finish,
+        out_shape=tuple(jax.ShapeDtypeStruct(shape, kind) for shape, kind in results),
         in_specs=[vmem] * 5,
-        out_specs=(vmem,) * 5,
+        out_specs=(hbm,) * 5,
+        scratch_shapes=[dma((5,))],
     )(*[pltpu.with_memory_space_constraint(value, pltpu.VMEM) for value in found])
     return (grid_out, grad_in, grad_bias.reshape(hidden_size), grad_out, grad_kernel)
 

time: 41.5 us -> 40.7 us (0.981)
  Pallas kernels: 40 us -> 39.2 us
    pallas_call x2, Pallas kernels: 40 us -> 39.2 us  [the longest x1 38.3 us: local(): pl.pallas_call(functools.partial(kernel, n_lat, n_lon, slots, batch, scal...]
where the time goes in v3:
time: 40.7 us; the launch traced here: 40.5 us
  Pallas kernels  39.2 us (96%)
  between operations  1.29 us (3%)
    pallas_call x1, Pallas kernels, local(): pl.pallas_call(functools.partial(kernel, n_lat, n_lon, slots, batch, scal...  38.3 us
    pallas_call x1, Pallas kernels, local(): pl.pallas_call(finish, out_shape=tuple((jax.ShapeDtypeStruct(shape, kind)...  0.86 us

profile of v3, /device:TPU:0, one launch (start us, length us, event | category | flops | bytes accessed | tf_op | source)
XLA Modules:
  0.0 40.5 jit_solution(150617394675817814)
XLA Ops:
  1.3 38.3 %shard_map.128 = (bf16[2,192,256]{2,1,0:T(8,128)(2,1)S(1)}, f32[128,256]{1,0:T(8,128)S(1)}, f32[1,256]{1,0:T(1,128)S(1)}, f32[256,256]{1,0:T(8,128)S(1)}, f32[9,256]{1,0:T(8,128)S(1)}) custom-call(bf16[1536,128]{1,0:T(8,128)(2,1)} %obs_h.1, s32[1,1536]{1,0:T(1,128)} %bitcast.5, s32[12,128]{1,0:T(8,128)} %bitcast.4, s32[1]{0:T(128)S(6)} %copy.14.count, ...), custom_call_target="tpu_custom_call" | custom-call | tf_op jit(solution)/shard_map/pallas_call | solution.py:690
  39.6 0.9 %shard_map.129 = (bf16[2,192,256]{2,1,0:T(8,128)(2,1)}, f32[128,256]{1,0:T(8,128)}, f32[1,256]{1,0:T(1,128)}, f32[256,256]{1,0:T(8,128)}, f32[9,256]{1,0:T(8,128)}) custom-call(bf16[2,192,256]{2,1,0:T(8,128)(2,1)S(1)} %get-tuple-element.15.refs_0_, f32[128,256]{1,0:T(8,128)S(1)} %get-tuple-element.16.refs_1_, f32[1,256]{1,0:T(1,128)S(1)} %get-tuple-element.17.refs_2_, ...), custom_call_target="tpu_custom_call" | custom-call | tf_op jit(solution)/shard_map/pallas_call | solution.py:725

commit v4 on v3

--- a/solution.py
+++ b/solution.py
@@ -15,7 +15,7 @@
 CURVE = math.sqrt(2.0 / math.pi)
 BEND = 0.044715
 EDGE = 8
-EARLY = 2
+EARLY = 1
 SEND = (("n", 0), ("n", 1), ("n", 2), ("n", 3), ("f", 0), ("f", 1), ("f", 2), ("f", 3))
 LATE = 2
 
@@ -40,9 +40,7 @@
     main_o, top_o, bot_o, sums_o, misc_o,
     meta, meta_r, slot_row, sbuf, rbuf, cot_s, cot_e, cot_r, cot_top, cot_bot, c32, adj_f, adj_b,
     dep, moved, con_s, con_e, gka, total, bias, tot_b, rs_r, z_s, z_r, fin_s, misc_s, misc_r, misc_z,
-    in_sem, meta_send, meta_recv, row_send, row_recv, cot_send, cot_recv, edge_send, top_recv, bot_recv,
-    con_send, con_recv, rim_send, rim_recv, rs_send, rs_recv, z_send, z_recv, ag_send, ag_recv,
-    mp_send, mp_recv, mz_send, mz_recv,
+    in_sem, sent, meta_recv, row_recv, near_recv, far_recv, top_recv, bot_recv, con_recv, rim_recv, rs_recv, z_recv, ag_recv, mp_recv, mz_recv,
 ):
     n = n_lat * n_lon
     lat, lon = lax.axis_index("lat"), lax.axis_index("lon")
@@ -96,7 +94,7 @@
         (owner_h, owner), (cell_h, cell), (obs_h, obs), (cot_h, cot),
         (w_in_h, w_in), (b_in_h, b_in), (w_out_h, w_out), (taps_h, taps),
     ]
-    fetches = [pltpu.make_async_copy(src, dst, in_sem.at[i]) for i, (src, dst) in enumerate(pairs)]
+    fetches = [pltpu.make_async_copy(src, dst, in_sem.at[min(i, 4)]) for i, (src, dst) in enumerate(pairs)]
     for fetch in fetches:
         fetch.start()
 
@@ -181,11 +179,15 @@
         for u in range(batch):
             sbuf[base + first + u] = rows[u * slots:(u + 1) * slots]
 
+    def slot(step):
+        quarter = step // (rounds // 4)
+        return jnp.where(quarter < 8 - LATE, quarter // 2, quarter - (8 - LATE) // 2)
+
     def ship_unit(off, where, base):
         to, target = where(off)
         at = base + off
-        remote(meta.at[target], meta_r.at[at], meta_send, meta_recv.at[at // batch], to).start()
-        remote(sbuf.at[at], rbuf.at[at], row_send, row_recv.at[at // batch], to).start()
+        remote(meta.at[target], meta_r.at[at], sent, meta_recv.at[slot(at // batch)], to).start()
+        remote(sbuf.at[at], rbuf.at[at], sent, row_recv.at[slot(at // batch)], to).start()
 
     rounds = peers // batch
 
@@ -224,8 +226,8 @@
             @pl.when(own)
             def _():
                 _, target = where(0)
-                pltpu.make_async_copy(meta.at[target], meta_r.at[base], meta_recv.at[base // batch]).start()
-                pltpu.make_async_copy(sbuf.at[base], rbuf.at[base], row_recv.at[base // batch]).start()
+                pltpu.make_async_copy(meta.at[target], meta_r.at[base], meta_recv.at[slot(base // batch)]).start()
+                pltpu.make_async_copy(sbuf.at[base], rbuf.at[base], row_recv.at[slot(base // batch)]).start()
 
             @pl.when(jnp.logical_not(own))
             def _():
@@ -274,7 +276,7 @@
             def go(e, to_tile, dst, sem):
                 to_lat = lax.rem(to_tile + deep, n_lat) if far_side else to_tile
                 for j in range(0, n_lon, 1 + far_side):
-                    remote(cot_e.at[e, j], dst.at[far_side], edge_send, sem.at[far_side], (to_lat, j)).start()
+                    remote(cot_e.at[e, j], dst.at[far_side], sent, sem.at[far_side], (to_lat, j)).start()
 
             @pl.when(jnp.logical_and(lon == n_lon - 1, lat < n_lat - 1))
             def _():
@@ -285,13 +287,13 @@
                 go(0, lat - 1, cot_bot, bot_recv)
 
         for step in range(1, n_lon):
-            remote(cot_s.at[hop(step)], cot_r.at[lon], cot_send, cot_recv.at[0], (lat, hop(step))).start()
+            remote(cot_s.at[hop(step)], cot_r.at[lon], sent, near_recv, (lat, hop(step))).start()
         cot_r[lon] = cot_s[lon]
         send_edges(0)
         for step in range(n_lon // 2):
             other = 2 * wrap(lon // 2 + step, n_lon // 2)
             remote(
-                cot_s.at[other], cot_r.at[n_lon + lon], cot_send, cot_recv.at[1], (far_lat, other)
+                cot_s.at[other], cot_r.at[n_lon + lon], sent, far_recv, (far_lat, other)
             ).start()
         send_edges(1)
 
@@ -311,9 +313,9 @@
 
     def cot_wait(s):
         if s == 0:
-            drain(cot_r.at[pl.ds(0, n_lon - 1)], cot_recv.at[0])
+            drain(cot_r.at[pl.ds(0, n_lon - 1)], near_recv)
         else:
-            drain(cot_r.at[pl.ds(0, n_lon)], cot_recv.at[1])
+            drain(cot_r.at[pl.ds(0, n_lon)], far_recv)
 
         @pl.when(tile_lat[s] > 0)
         def _():
@@ -362,9 +364,8 @@
         first, size = step * batch, count * batch
         s = first // peers
         with scope("rowwait"):
-            for i in range(count):
-                drain(meta_r.at[pl.ds(first + i * batch, batch)], meta_recv.at[step + i])
-                drain(rbuf.at[pl.ds(first + i * batch, batch)], row_recv.at[step + i])
+            drain(meta_r.at[pl.ds(first, size)], meta_recv.at[slot(step)])
+            drain(rbuf.at[pl.ds(first, size)], row_recv.at[slot(step)])
         rows = jnp.concatenate([rbuf[first + q] for q in range(size)], axis=0)
         codes = jnp.concatenate([meta_r[first + q][:, 0:slots] for q in range(size)], axis=1)
         pick = (codes == iota((cells, size * slots), 0) + 1).astype(F32).astype(BF16)
@@ -423,7 +424,7 @@
         for p in range(n_lon):
             tot_b[p] = total[p * piece:(p + 1) * piece, :].astype(BF16)
         for step in range(1, n_lon):
-            remote(tot_b.at[hop(step)], rs_r.at[lon], rs_send, rs_recv, (lat, hop(step))).start()
+            remote(tot_b.at[hop(step)], rs_r.at[lon], sent, rs_recv, (lat, hop(step))).start()
 
     def spread(h):
         def turn_row(m, carry):
@@ -470,14 +471,14 @@
     def send_strip(h, step):
         where = lon if h == 0 else n_lon + lon // 2
         remote(
-            con_s.at[h, hop(step)], main_o.at[where], con_send, con_recv, (tile_lat[h], hop(step))
+            con_s.at[h, hop(step)], main_o.at[where], sent, con_recv, (tile_lat[h], hop(step))
         ).start()
 
     def rim_copy(h, e):
         where = lon if h == 0 else n_lon + lon // 2
         if e == 0:
-            return remote(con_e.at[h, 0], bot_o.at[where], rim_send, rim_recv.at[0], (tile_lat[h] - 1, n_lon - 1))
-        return remote(con_e.at[h, 1], top_o.at[where], rim_send, rim_recv.at[1], (tile_lat[h] + 1, 0))
+            return remote(con_e.at[h, 0], bot_o.at[where], sent, rim_recv, (tile_lat[h] - 1, n_lon - 1))
+        return remote(con_e.at[h, 1], top_o.at[where], sent, rim_recv, (tile_lat[h] + 1, 0))
 
     def rims(h, act):
         @pl.when(tile_lat[h] > 0)
@@ -511,7 +512,7 @@
             [bias[...]] + grads + [jnp.zeros((spare, channels), F32)], axis=0
         ).astype(BF16)
         for step in range(1, n_lon):
-            remote(misc_s, misc_r.at[lon], mp_send, mp_recv, (lat, hop(step))).start()
+            remote(misc_s, misc_r.at[lon], sent, mp_recv, (lat, hop(step))).start()
         misc_r[lon] = misc_s[...]
 
     with scope("rswait"):
@@ -523,7 +524,7 @@
             part = part + rs_r[p].astype(F32)
         z_s[...] = part.astype(BF16)
         for step in range(1, n_lat):
-            remote(z_s, z_r.at[lat], z_send, z_recv, (wrap(lat + step, n_lat), lon)).start()
+            remote(z_s, z_r.at[lat], sent, z_recv, (wrap(lat + step, n_lat), lon)).start()
         z_r[lat] = z_s[...]
 
         @pl.when(dense)
@@ -542,7 +543,7 @@
             part = part + misc_r[p].astype(F32)
         misc_z[...] = part.astype(BF16)
         for step in range(1, n_lat):
-            remote(misc_z, misc_o.at[lat], mz_send, mz_recv, (wrap(lat + step, n_lat), lon)).start()
+            remote(misc_z, misc_o.at[lat], sent, mz_recv, (wrap(lat + step, n_lat), lon)).start()
         misc_o[lat] = misc_z[...]
 
     with scope("zwait"):
@@ -553,7 +554,7 @@
             part = part + z_r[p].astype(F32)
         fin_s[...] = part.astype(BF16)
         for step in range(1, n_lon):
-            remote(fin_s, sums_o.at[lon], ag_send, ag_recv, (lat, hop(step))).start()
+            remote(fin_s, sums_o.at[lon], sent, ag_recv, (lat, hop(step))).start()
         sums_o[lon] = fin_s[...]
 
     with scope("mzwait"):
@@ -563,11 +564,11 @@
 
         @pl.when(has_top)
         def _():
-            drain(top_o, rim_recv.at[1])
+            drain(top_o, rim_recv)
 
         @pl.when(has_bot)
         def _():
-            drain(bot_o, rim_recv.at[0])
+            drain(bot_o, rim_recv)
     with scope("grid"):
         value = misc_o[0].astype(F32)
         for z in range(1, n_lat):
@@ -615,42 +616,42 @@
                     ref[begin - low:end - low, :] = value[begin - start:end - start]
 
     with scope("final"):
-        drain(sbuf.at[pl.ds(0, 2 * peers - 2)], row_send)
-        drain(meta_r.at[pl.ds(0, 2 * peers - 2)], meta_send)
+        drain(sbuf.at[pl.ds(0, 2 * peers - 2)], sent)
+        drain(meta_r.at[pl.ds(0, 2 * peers - 2)], sent)
 
         @pl.when(jnp.logical_not(dense))
         def _():
-            drain(sbuf.at[0], row_send)
-            drain(meta_r.at[0], meta_send)
-
-        drain(cot_r.at[pl.ds(0, holders - 1)], cot_send)
+            drain(sbuf.at[0], sent)
+            drain(meta_r.at[0], sent)
+
+        drain(cot_r.at[pl.ds(0, holders - 1)], sent)
 
         @pl.when(jnp.logical_and(lon == n_lon - 1, lat < n_lat - 1))
         def _():
-            drain(top_o, edge_send)
+            drain(top_o, sent)
 
         @pl.when(jnp.logical_and(lon == 0, lat > 0))
         def _():
-            drain(top_o, edge_send)
-
-        drain(main_o.at[pl.ds(0, n_lon - 1)], con_send)
+            drain(top_o, sent)
+
+        drain(main_o.at[pl.ds(0, n_lon - 1)], sent)
         rims(0, lambda copy: copy.wait_send())
 
         @pl.when(dense)
         def _():
-            drain(main_o.at[pl.ds(0, n_lon)], con_send)
+            drain(main_o.at[pl.ds(0, n_lon)], sent)
             rims(1, lambda copy: copy.wait_send())
 
-        drain(rs_r.at[pl.ds(0, n_lon - 1)], rs_send)
-        drain(misc_r.at[pl.ds(0, n_lon - 1)], mp_send)
-        drain(z_r.at[pl.ds(0, n_lat - 1)], z_send)
-        drain(misc_o.at[pl.ds(0, n_lat - 1)], mz_send)
-        drain(sums_o.at[pl.ds(0, n_lon - 1)], ag_send)
+        drain(rs_r.at[pl.ds(0, n_lon - 1)], sent)
+        drain(misc_r.at[pl.ds(0, n_lon - 1)], sent)
+        drain(z_r.at[pl.ds(0, n_lat - 1)], sent)
+        drain(misc_o.at[pl.ds(0, n_lat - 1)], sent)
+        drain(sums_o.at[pl.ds(0, n_lon - 1)], sent)
 
 
 def finish(*refs):
     sem, half = refs[-1], (len(refs) - 1) // 2
-    copies = [pltpu.make_async_copy(refs[i], refs[half + i], sem.at[i]) for i in range(half)]
+    copies = [pltpu.make_async_copy(refs[i], refs[half + i], sem) for i in range(half)]
     for copy in copies:
         copy.start()
     for copy in copies:
@@ -710,9 +711,8 @@
             V((n_lon, piece, channels), BF16), V((n_lon, piece, channels), BF16),
             V((piece, channels), BF16), V((n_lat, piece, channels), BF16), V((piece, channels), BF16),
             V((misc_rows, channels), BF16), V((n_lon, misc_rows, channels), BF16), V((misc_rows, channels), BF16),
-            dma((8,)), dma, dma((n // batch,)), dma, dma((n // batch,)), dma, dma((2,)), dma, dma((2,)), dma((2,)),
-            dma, dma, dma, dma((2,)), dma, dma, dma, dma, dma, dma,
-            dma, dma, dma, dma,
+            dma((5,)), dma, dma((4 + LATE // 2,)), dma((4 + LATE // 2,)), dma, dma, dma((2,)), dma((2,)),
+            dma, dma, dma, dma, dma, dma, dma,
         ],
         compiler_params=pltpu.CompilerParams(
             collective_id=0, has_side_effects=True, vmem_limit_bytes=48 * 1024 * 1024
@@ -727,7 +727,7 @@
         out_shape=tuple(jax.ShapeDtypeStruct(shape, kind) for shape, kind in results),
         in_specs=[vmem] * 5,
         out_specs=(hbm,) * 5,
-        scratch_shapes=[dma((5,))],
+        scratch_shapes=[dma],
     )(*[pltpu.with_memory_space_constraint(value, pltpu.VMEM) for value in found])
     return (grid_out, grad_in, grad_bias.reshape(hidden_size), grad_out, grad_kernel)
 

time: 40.7 us -> 40.3 us (level)
  no operation moved by 1% of the time
where the time goes in v4:
time: 40.3 us; the launch traced here: 40.1 us
  Pallas kernels  38.8 us (96%)
  between operations  1.29 us (3%)
    pallas_call x1, Pallas kernels, local(): pl.pallas_call(functools.partial(kernel, n_lat, n_lon, slots, batch, scal...  38 us
    pallas_call x1, Pallas kernels, local(): pl.pallas_call(finish, out_shape=tuple((jax.ShapeDtypeStruct(shape, kind)...  0.83 us

profile of v4, /device:TPU:0, one launch (start us, length us, event | category | flops | bytes accessed | tf_op | source)
XLA Modules:
  0.0 40.1 jit_solution(12906382504322199677)
XLA Ops:
  1.3 38.0 %shard_map.128 = (bf16[2,192,256]{2,1,0:T(8,128)(2,1)S(1)}, f32[128,256]{1,0:T(8,128)S(1)}, f32[1,256]{1,0:T(1,128)S(1)}, f32[256,256]{1,0:T(8,128)S(1)}, f32[9,256]{1,0:T(8,128)S(1)}) custom-call(bf16[1536,128]{1,0:T(8,128)(2,1)} %obs_h.1, s32[1,1536]{1,0:T(1,128)} %bitcast.5, s32[12,128]{1,0:T(8,128)} %bitcast.4, s32[1]{0:T(128)S(6)} %copy.14.count, ...), custom_call_target="tpu_custom_call" | custom-call | tf_op jit(solution)/shard_map/pallas_call | solution.py:691
  39.2 0.8 %shard_map.129 = (bf16[2,192,256]{2,1,0:T(8,128)(2,1)}, f32[128,256]{1,0:T(8,128)}, f32[1,256]{1,0:T(1,128)}, f32[256,256]{1,0:T(8,128)}, f32[9,256]{1,0:T(8,128)}) custom-call(bf16[2,192,256]{2,1,0:T(8,128)(2,1)S(1)} %get-tuple-element.15.refs_0_, f32[128,256]{1,0:T(8,128)S(1)} %get-tuple-element.16.refs_1_, f32[1,256]{1,0:T(1,128)S(1)} %get-tuple-element.17.refs_2_, ...), custom_call_target="tpu_custom_call" | custom-call | tf_op jit(solution)/shard_map/pallas_call | solution.py:725

commit v5 on v4

--- a/solution.py
+++ b/solution.py
@@ -295,11 +295,13 @@
             remote(
                 cot_s.at[other], cot_r.at[n_lon + lon], sent, far_recv, (far_lat, other)
             ).start()
-        send_edges(1)
 
         loops(send_order[:ready], ship_step)
     with scope("prep2"):
-        loops(send_order[ready:], both_step)
+        cut = 2 * (rounds // 4)
+        loops(send_order[ready:cut], both_step)
+        send_edges(1)
+        loops(send_order[cut:], both_step)
 
     with scope("clear"):
         for s in range(2):

time: 40.3 us -> 40.1 us (level)
  no operation moved by 1% of the time
where the time goes in v5:
time: 40.1 us; the launch traced here: 39.9 us
  Pallas kernels  38.6 us (96%)
  between operations  1.29 us (3%)
    pallas_call x1, Pallas kernels, local(): pl.pallas_call(functools.partial(kernel, n_lat, n_lon, slots, batch, scal...  37.8 us
    pallas_call x1, Pallas kernels, local(): pl.pallas_call(finish, out_shape=tuple((jax.ShapeDtypeStruct(shape, kind)...  0.83 us

profile of v5, /device:TPU:0, one launch (start us, length us, event | category | flops | bytes accessed | tf_op | source)
XLA Modules:
  0.0 39.9 jit_solution(1593473631182097300)
XLA Ops:
  1.3 37.8 %shard_map.128 = (bf16[2,192,256]{2,1,0:T(8,128)(2,1)S(1)}, f32[128,256]{1,0:T(8,128)S(1)}, f32[1,256]{1,0:T(1,128)S(1)}, f32[256,256]{1,0:T(8,128)S(1)}, f32[9,256]{1,0:T(8,128)S(1)}) custom-call(bf16[1536,128]{1,0:T(8,128)(2,1)} %obs_h.1, s32[1,1536]{1,0:T(1,128)} %bitcast.5, s32[12,128]{1,0:T(8,128)} %bitcast.4, s32[1]{0:T(128)S(6)} %copy.14.count, ...), custom_call_target="tpu_custom_call" | custom-call | tf_op jit(solution)/shard_map/pallas_call | solution.py:693
  39.0 0.8 %shard_map.129 = (bf16[2,192,256]{2,1,0:T(8,128)(2,1)}, f32[128,256]{1,0:T(8,128)}, f32[1,256]{1,0:T(1,128)}, f32[256,256]{1,0:T(8,128)}, f32[9,256]{1,0:T(8,128)}) custom-call(bf16[2,192,256]{2,1,0:T(8,128)(2,1)S(1)} %get-tuple-element.15.refs_0_, f32[128,256]{1,0:T(8,128)S(1)} %get-tuple-element.16.refs_1_, f32[1,256]{1,0:T(1,128)S(1)} %get-tuple-element.17.refs_2_, ...), custom_call_target="tpu_custom_call" | custom-call | tf_op jit(solution)/shard_map/pallas_call | solution.py:727
